TPU v7x, 64 devices: a 2x2x8 block of a 4x4x8 slice. The times are simulated.
64 devices in a mesh: rep: 4 (over x, y), dp: 16 (over z, core).
Axes of the slice: x: 2, y: 2, z: 8, core: 2. Of those that a mesh axis runs over, the one named last changes fastest.
The devices are a block of a 4x4x8 slice.
Arguments:
- g_w_gate: bfloat16 [64, 2, 640, 2048], P(('rep', 'dp')), parts along dimension 0
- g_w_up: bfloat16 [64, 2, 640, 2048], P(('rep', 'dp')), parts along dimension 0
- g_w_down: bfloat16 [64, 2, 2048, 640], P(('rep', 'dp')), parts along dimension 0
- w_gate: bfloat16 [2, 640, 2048], replicated
- w_up: bfloat16 [2, 640, 2048], replicated
- w_down: bfloat16 [2, 2048, 640], replicated
- m_w_gate: float32 [2, 640, 2048], P(None, 'dp')
- m_w_up: float32 [2, 640, 2048], P(None, 'dp')
- m_w_down: float32 [2, 2048, 640], P(None, 'dp')
- v_w_gate: float32 [2, 640, 2048], P(None, 'dp')
- v_w_up: float32 [2, 640, 2048], P(None, 'dp')
- v_w_down: float32 [2, 2048, 640], P(None, 'dp')
Outputs:
- output 1: bfloat16 [8, 640, 2048], P('rep'), parts along dimension 0
- output 2: bfloat16 [8, 640, 2048], P('rep'), parts along dimension 0
- output 3: bfloat16 [8, 2048, 640], P('rep'), parts along dimension 0
- output 4: float32 [8, 640, 2048], P('rep', 'dp'), parts along dimension 0
- output 5: float32 [8, 640, 2048], P('rep', 'dp'), parts along dimension 0
- output 6: float32 [8, 2048, 640], P('rep', 'dp'), parts along dimension 0
- output 7: float32 [8, 640, 2048], P('rep', 'dp'), parts along dimension 0
- output 8: float32 [8, 640, 2048], P('rep', 'dp'), parts along dimension 0
- output 9: float32 [8, 2048, 640], P('rep', 'dp'), parts along dimension 0
There are 4 independent parts. A program takes and returns all parts, laid end to end along the dimension named above; an argument that names none is the same for every part.
All inputs are finite; a program needn't handle non-finite values.
Results may differ from a plain program's by a relative error of at most 0.022.
Values are sent between devices in bfloat16 or wider.
A program may use at most 768 MiB of HBM per device.

v0:
```python
import jax
import jax.numpy as jnp
from jax import lax
from jax.sharding import PartitionSpec as P


def adamw(w, m, v, g):
    m = 0.9 * m + 0.1 * g
    v = 0.95 * v + 0.05 * g * g
    step = m * lax.rsqrt(v + 1e-8) + 0.1 * w
    return (w - 0.02 * step).astype(jnp.bfloat16), m, v


def solution(mesh):
    def step(*arrays):
        terms, weights, m, v = (arrays[i : i + 3] for i in (0, 3, 6, 9))
        gradients = [lax.psum_scatter(t[0], "dp", scatter_dimension=1, tiled=True).astype(jnp.float32) for t in terms]
        me = lax.axis_index("dp")
        own = [lax.dynamic_slice_in_dim(w, me * one.shape[1], one.shape[1], 1).astype(jnp.float32) for w, one in zip(weights, m, strict=True)]
        new = [adamw(w, m, v, g) for w, m, v, g in zip(own, m, v, gradients, strict=True)]
        whole = [lax.all_gather(one[0], "dp", axis=1, tiled=True) for one in new]
        return (*whole, *(one[1] for one in new), *(one[2] for one in new))

    all_of, cut = P(None, None, None), P(None, "dp", None)
    return jax.shard_map(
        step,
        mesh=mesh,
        in_specs=(P(("rep", "dp"), None, None, None),) * 3 + (all_of,) * 3 + (cut,) * 6,
        out_specs=(P("rep", None, None),) * 3 + (P("rep", "dp", None),) * 6,
        check_vma=False,
    )
```

profile of v0, /device:TPU:21, one launch (start us, length us, event | category | flops | bytes accessed | tf_op | source)
XLA Modules:
  0.0 343.8 jit_solution(15327807392448866905)
XLA Ops:
  7.2 0.1 reduce-scatter.8.cloned.1.call-start
  7.3 0.7 reduce-scatter.8.cloned.1.call-update
  8.0 0.1 reduce-scatter.10.cloned.1.call-start
  8.1 10.2 %copy.21 = bf16[2,640,2048]{2,0,1:T(2,128)(2,1)} copy(bf16[2,640,2048]{2,1,0:T(8,128)(2,1)} %bitcast.15) | data formatting | bytes 10485760
  18.3 8.2 %copy.25 = bf16[80,8,2,2048]{3,1,2,0:T(8,128)(2,1)} copy(bf16[80,8,2,2048]{3,2,1,0:T(2,128)(2,1)} %bitcast.13) | data formatting | bytes 10485760
  26.4 0.1 reduce-scatter.10.cloned.1.call-update
  26.5 0.2 reduce-scatter.12.cloned.1.call-start
  26.8 10.2 %copy.23 = bf16[2,640,2048]{2,0,1:T(2,128)(2,1)} copy(bf16[2,640,2048]{2,1,0:T(8,128)(2,1)} %bitcast.16) | data formatting | bytes 10485760
  37.0 8.2 %copy.26 = bf16[80,8,2,2048]{3,1,2,0:T(8,128)(2,1)} copy(bf16[80,8,2,2048]{3,2,1,0:T(2,128)(2,1)} %bitcast.14) | data formatting | bytes 10485760
  45.2 0.1 reduce-scatter.12.cloned.1.call-update
  45.2 0.0 copy-start.5
  45.2 0.1 all-gather.8.cloned.1.call-start
  45.3 28.5 %reduce-scatter.8.cloned.1.call-done = bf16[2,128,640]{2,1,0:T(8,128)(2,1)} async-done(((bf16[2,2048,640]{2,1,0:T(8,128)(2,1)}), bf16[2,128,640]{2,1,0:T(8,128)(2,1)}) %reduce-scatter.8.cloned.1.call-update) | async-done | bytes 327696 | tf_op jit(solution)/shard_map/reduce_scatter | solution.py:17
  73.9 2.4 fusion.10
  76.3 0.1 all-gather.8.cloned.1.call-update
  76.3 0.1 all-gather.4.cloned.1.call-start
  76.4 61.0 %reduce-scatter.10.cloned.1.call-done = bf16[40,4096]{1,0:T(8,128)(2,1)} async-done(((bf16[640,4096]{1,0:T(8,128)(2,1)}), bf16[40,4096]{1,0:T(8,128)(2,1)}) %reduce-scatter.10.cloned.1.call-update) | async-done | bytes 327696
  137.4 1.2 reshape.19
  138.6 2.4 fusion.2
  141.0 0.1 all-gather.4.cloned.1.call-update
  141.1 0.1 all-gather.6.cloned.1.call-start
  141.2 59.8 %reduce-scatter.12.cloned.1.call-done = bf16[40,4096]{1,0:T(8,128)(2,1)} async-done(((bf16[640,4096]{1,0:T(8,128)(2,1)}), bf16[40,4096]{1,0:T(8,128)(2,1)}) %reduce-scatter.12.cloned.1.call-update) | async-done | bytes 327696
  201.0 1.2 reshape.21
  202.2 0.0 copy-done.5
  202.2 2.4 fusion.6
  204.6 0.1 all-gather.6.cloned.1.call-update
  204.7 40.1 %all-gather.8.cloned.1.call-done = bf16[2,2048,640]{2,1,0:T(8,128)(2,1)} async-done(((bf16[2,128,640]{2,1,0:T(8,128)(2,1)}), bf16[2,2048,640]{2,1,0:T(8,128)(2,1)}) %all-gather.8.cloned.1.call-update) | async-done | bytes 5242896 | tf_op jit(solution)/shard_map/all_gather | solution.py:21
  244.7 40.7 %all-gather.4.cloned.1.call-done = bf16[2,640,2048]{2,1,0:T(8,128)(2,1)} async-done(((bf16[2,40,2048]{2,1,0:T(8,128)(2,1)}), bf16[2,640,2048]{2,1,0:T(8,128)(2,1)}) %all-gather.4.cloned.1.call-update) | async-done | bytes 5242896 | tf_op jit(solution)/shard_map/all_gather | solution.py:21
  285.4 40.7 %all-gather.6.cloned.1.call-done = bf16[2,640,2048]{2,1,0:T(8,128)(2,1)} async-done(((bf16[2,40,2048]{2,1,0:T(8,128)(2,1)}), bf16[2,640,2048]{2,1,0:T(8,128)(2,1)}) %all-gather.6.cloned.1.call-update) | async-done | bytes 5242896 | tf_op jit(solution)/shard_map/all_gather | solution.py:21
  326.1 6.2 %copy.38 = bf16[2,640,2048]{2,1,0:T(8,128)(2,1)} copy(bf16[2,640,2048]{2,1,0:T(8,128)(2,1)} %all-gather.4.cloned.1.call-done) | data formatting | bytes 10485760
  332.2 2.4 copy.39
  334.6 2.4 copy.40
  (17 shorter events, 0.0 us)
Async XLA Ops:
  7.2 66.7 %reduce-scatter.8.cloned.1.call-start = ((), (), s32[]{:S(2)}) async-start(), calls=%async_computation.5 | async-start | bytes 5570560 | tf_op jit(solution)/shard_map/reduce_scatter | solution.py:17
  8.0 129.4 %reduce-scatter.10.cloned.1.call-start = ((), (), s32[]{:S(2)}) async-start(), calls=%async_computation.7 | async-start | bytes 5570560
  26.5 174.4 %reduce-scatter.12.cloned.1.call-start = ((), (), s32[]{:S(2)}) async-start(), calls=%async_computation.8 | async-start | bytes 5570560
  45.2 28.7 %copy-start.1 = (f32[2,128,640]{2,1,0:T(8,128)S(1)}, f32[2,128,640]{2,1,0:T(8,128)}, u32[]{:S(2)}) copy-start(f32[2,128,640]{2,1,0:T(8,128)} %param.23) | copy-start | bytes 1966084
  45.2 28.7 %copy-start.2 = (f32[2,128,640]{2,1,0:T(8,128)S(1)}, f32[2,128,640]{2,1,0:T(8,128)}, u32[]{:S(2)}) copy-start(f32[2,128,640]{2,1,0:T(8,128)} %param.20) | copy-start | bytes 1966084
  45.2 93.5 %copy-start.3 = (f32[2,40,2048]{2,1,0:T(8,128)S(1)}, f32[2,40,2048]{2,1,0:T(8,128)}, u32[]{:S(2)}) copy-start(f32[2,40,2048]{2,1,0:T(8,128)} %param.21) | copy-start | bytes 1966084
  45.2 93.5 %copy-start.4 = (f32[2,40,2048]{2,1,0:T(8,128)S(1)}, f32[2,40,2048]{2,1,0:T(8,128)}, u32[]{:S(2)}) copy-start(f32[2,40,2048]{2,1,0:T(8,128)} %param.18) | copy-start | bytes 1966084
  45.2 156.9 %copy-start.5 = (f32[2,40,2048]{2,1,0:T(8,128)S(1)}, f32[2,40,2048]{2,1,0:T(8,128)}, u32[]{:S(2)}) copy-start(f32[2,40,2048]{2,1,0:T(8,128)} %param.22) | copy-start | bytes 1966084
  45.2 199.5 %all-gather.8.cloned.1.call-start = ((), (), s32[]{:S(2)}) async-start(), calls=%async_computation.6 | async-start | bytes 5570560 | tf_op jit(solution)/shard_map/all_gather | solution.py:21
  76.3 125.9 %copy-start.6 = (f32[2,40,2048]{2,1,0:T(8,128)S(1)}, f32[2,40,2048]{2,1,0:T(8,128)}, u32[]{:S(2)}) copy-start(f32[2,40,2048]{2,1,0:T(8,128)} %param.19) | copy-start | bytes 1966084
  76.3 209.1 %all-gather.4.cloned.1.call-start = ((), (), s32[]{:S(2)}) async-start(), calls=%async_computation.3 | async-start | bytes 5570560 | tf_op jit(solution)/shard_map/all_gather | solution.py:21
  141.1 185.0 %all-gather.6.cloned.1.call-start = ((), (), s32[]{:S(2)}) async-start(), calls=%async_computation.4 | async-start | bytes 5570560 | tf_op jit(solution)/shard_map/all_gather | solution.py:21
  326.1 6.2 %copy-start = (bf16[2,640,2048]{2,1,0:T(8,128)(2,1)S(1)}, bf16[2,640,2048]{2,1,0:T(8,128)(2,1)}, u32[]{:S(2)}) copy-start(bf16[2,640,2048]{2,1,0:T(8,128)(2,1)} %all-gather.6.cloned.1.call-done) | copy-start | bytes 15728644
  326.1 8.5 %slice-start = ((s8[5242880]{0:T(1024)(128)(4,1)}), s8[4194304]{0:T(1024)(128)(4,1)S(1)}, s32[]{:S(2)}) async-start(s8[5242880]{0:T(1024)(128)(4,1)} %bitcast.18), calls=%async_computation.9 | async-start | bytes 8388608
  332.2 2.4 slice-start.1
Sparse Core Ops, SparseCore 0:
  10.4 63.4 reduce-scatter.7
  76.8 60.5 reduce-scatter.9
  140.3 60.5 reduce-scatter.11
  202.5 42.2 all-gather.7
  246.8 38.5 all-gather.3
  287.5 38.5 all-gather.5
where the time goes:
time: 344 us
  waiting for transfers between devices  272 us (79%)
  local copies, waits for them, and re-layouts  50.1 us (15%)
  between operations  14.2 us (4%)
  other arithmetic  7.2 us (2%)
    unnamed x8, waiting for transfers between devices  122 us
    all_gather x3, waiting for transfers between devices, step(): whole = [lax.all_gather(one[0], 'dp', axis=1, tiled=True) for one in new]  121 us
    unnamed x27, local copies, waits for them, and re-layouts  50.1 us
    reduce_scatter x1, waiting for transfers between devices, step(): lax.psum_scatter(t[0], 'dp', scatter_dimension=1, tiled=True)  28.5 us
    convert_element_type x3, other arithmetic, adamw(): return ((w - 0.02 * step).astype(jnp.bfloat16), m, v)  7.2 us
  transfers between devices with their start and end apart: 6, of which 6 were waited for; matrix products, arithmetic and copies ran while one was open for 14% of the time, Pallas kernels for 0%

commit v1 on v0

v1 whole, which is shorter than its diff:
```python
import functools

import jax
import jax.numpy as jnp
from jax import lax
from jax.experimental import pallas as pl
from jax.experimental.pallas import tpu as pltpu
from jax.sharding import PartitionSpec as P

MESH = pl.DeviceIdType.MESH
CORES = 2
SUBLANES = 8


def adamw(w, m, v, g):
    m = 0.9 * m + 0.1 * g
    v = 0.95 * v + 0.05 * g * g
    step = m * lax.rsqrt(v + 1e-8) + 0.1 * w
    return (w - 0.02 * step).astype(jnp.bfloat16), m, v


def kernel(n, chips, layers, *refs):
    refs = iter(refs)
    take = lambda count: [next(refs) for _ in range(count)]
    g, w, m_in, v_in = take(n), take(n), take(n), take(n)
    new_w, new_m, new_v = take(n), take(n), take(n)
    own, pair, ring, old_w = take(n), take(n), take(n), take(n)
    (load_sem, state_sem, pair_recv, ring_recv, gather_recv, share_recv, pair_send, ring_send, gather_send, share_send) = take(10)

    me = lax.axis_index("dp")
    chip, core = me // CORES, me % CORES
    other = 1 - core
    partner = {"dp": chip * CORES + other}
    right = {"dp": (chip + 1) % chips * CORES + core}
    left = {"dp": (chip + chips - 1) % chips * CORES + core}
    ahead = [right if layer % 2 == 0 else left for layer in range(layers)]

    def block(step, layer):
        return (chip + chips - 1 - step if layer % 2 == 0 else chip + 1 + step) % chips

    def source(step, layer):
        return (chip + chips - step if layer % 2 == 0 else chip + step) % chips

    pieces = [(a, layer) for a in range(n) for layer in range(layers)]

    def load(a, step, layer):
        return pltpu.make_async_copy(g[a].at[layer, block(step, layer), core], own[a].at[step, layer], load_sem.at[a, step, layer])

    def swap(a, step, layer):
        return pltpu.make_async_remote_copy(
            g[a].at[layer, block(step, layer), other], pair[a].at[step, layer], pair_send.at[a], pair_recv.at[a, step, layer], partner, MESH
        )

    def hop(a, step, layer):
        return pltpu.make_async_remote_copy(
            own[a].at[step, layer], ring[a].at[step, layer], ring_send.at[a], ring_recv.at[a, step, layer], ahead[layer], MESH
        )

    def spread(a, step, layer):
        here = new_w[a].at[layer, source(step, layer), core]
        return pltpu.make_async_remote_copy(here, here, gather_send.at[a], gather_recv.at[a, step, layer], ahead[layer], MESH)

    def share(a, step, layer):
        here = new_w[a].at[layer, source(step, layer), core]
        return pltpu.make_async_remote_copy(here, here, share_send.at[a], share_recv.at[a], partner, MESH)

    def states(a):
        return [
            pltpu.make_async_copy(m_in[a], new_m[a], state_sem.at[0, a]),
            pltpu.make_async_copy(v_in[a], new_v[a], state_sem.at[1, a]),
        ] + [pltpu.make_async_copy(w[a].at[layer, chip, core], old_w[a].at[layer], state_sem.at[2 + layer, a]) for layer in range(layers)]

    @pl.loop(0, chips)
    def _(step):
        for a, layer in pieces:
            load(a, step, layer).start()

    barrier = pltpu.get_barrier_semaphore()
    for device in (partner, right, left):
        pl.semaphore_signal(barrier, inc=1, device_id=device, device_id_type=MESH)
    pl.semaphore_wait(barrier, 3)

    @pl.loop(0, chips)
    def _(step):
        for a, layer in pieces:
            swap(a, step, layer).start()

    for a in range(n):
        for copy in states(a):
            copy.start()

    def total(a, step, layer, i, arrived):
        t = own[a][step, layer, i].astype(jnp.float32) + pair[a][step, layer, i].astype(jnp.float32)
        if arrived is not None:
            t = t + ring[a][arrived, layer, i].astype(jnp.float32)
        return t

    def pair_sum(step, arrived):
        for a, layer in pieces:
            load(a, step, layer).wait()
            swap(a, step, layer).wait_recv()
            if arrived is not None:
                hop(a, arrived, layer).wait_recv()

            @pl.loop(0, own[a].shape[2])
            def _(i):
                own[a][step, layer, i] = total(a, step, layer, i, arrived).astype(jnp.bfloat16)

            hop(a, step, layer).start()

    pair_sum(0, None)

    @pl.loop(1, chips - 1)
    def _(step):
        pair_sum(step, step - 1)

    last = chips - 1
    for a in range(n):
        for copy in states(a):
            copy.wait()
    for a, layer in pieces:
        load(a, last, layer).wait()
        swap(a, last, layer).wait_recv()
        hop(a, last - 1, layer).wait_recv()

        @pl.loop(0, own[a].shape[2])
        def _(i):
            grad = total(a, last, layer, i, last - 1).astype(jnp.bfloat16).astype(jnp.float32)
            new = adamw(old_w[a][layer, i].astype(jnp.float32), new_m[a][layer, i], new_v[a][layer, i], grad)
            new_w[a][layer, chip, core, i], new_m[a][layer, i], new_v[a][layer, i] = new

        spread(a, 0, layer).start()
        share(a, 0, layer).start()

    @pl.loop(1, chips - 1)
    def _(step):
        for a, layer in pieces:
            spread(a, step - 1, layer).wait_recv()
            spread(a, step, layer).start()
            share(a, step, layer).start()

    for a, layer in pieces:
        spread(a, last - 1, layer).wait_recv()
        share(a, last, layer).start()

    for a in range(n):
        pltpu.make_async_remote_copy(pair[a], pair[a], pair_send.at[a], share_recv.at[a], partner, MESH).wait_send()
        pltpu.make_async_remote_copy(ring[a], ring[a], ring_send.at[a], share_recv.at[a], partner, MESH).wait_send()
        pltpu.make_async_remote_copy(ring[a], ring[a], gather_send.at[a], share_recv.at[a], partner, MESH).wait_send()
        pltpu.make_async_remote_copy(pair[a], pair[a], share_send.at[a], share_recv.at[a], partner, MESH).wait()


def solution(mesh):
    chips = mesh.shape["dp"] // CORES

    def step(*arrays):
        terms, weights, m, v = (arrays[i : i + 3] for i in (0, 3, 6, 9))
        n, layers = len(terms), weights[0].shape[0]
        tiles = [(one.shape[1] // SUBLANES, SUBLANES, one.shape[2]) for one in m]
        whole = [(layers, chips, CORES, *tile) for tile in tiles]
        state = [(layers, *tile) for tile in tiles]
        operands = [one.reshape(shape) for one, shape in zip(terms, whole, strict=True)]
        operands += [one.reshape(shape) for one, shape in zip(weights, whole, strict=True)]
        operands += [one.reshape(shape) for part in (m, v) for one, shape in zip(part, state, strict=True)]
        sems = lambda *shape: pltpu.SemaphoreType.DMA(shape)
        vmem = lambda lead, dtype: [pltpu.VMEM((*lead, *tile), dtype) for tile in tiles]
        out = pl.pallas_call(
            functools.partial(kernel, n, chips, layers),
            out_shape=[pltpu.VMEM(shape, jnp.bfloat16) for shape in whole] + [pltpu.VMEM(shape, jnp.float32) for shape in state] * 2,
            in_specs=[pl.BlockSpec(memory_space=pl.ANY)] * len(operands),
            out_specs=[pl.BlockSpec(memory_space=pltpu.VMEM)] * (3 * n),
            scratch_shapes=[
                *vmem((chips, layers), jnp.bfloat16),
                *vmem((chips, layers), jnp.bfloat16),
                *vmem((chips - 1, layers), jnp.bfloat16),
                *vmem((layers,), jnp.bfloat16),
                sems(n, chips, layers),
                sems(2 + layers, n),
                sems(n, chips, layers),
                sems(n, chips - 1, layers),
                sems(n, chips - 1, layers),
                sems(n),
                sems(n),
                sems(n),
                sems(n),
                sems(n),
            ],
            compiler_params=pltpu.CompilerParams(collective_id=0, has_side_effects=True, vmem_limit_bytes=40 << 20),
            name="step",
        )(*operands)
        return tuple(one.reshape(like.shape) for one, like in zip(out, (*weights, *m, *v), strict=True))

    all_of, cut = P(None, None, None), P(None, "dp", None)
    return jax.shard_map(
        step,
        mesh=mesh,
        in_specs=(P(("rep", "dp"), None, None, None),) * 3 + (all_of,) * 3 + (cut,) * 6,
        out_specs=(P("rep", None, None),) * 3 + (P("rep", "dp", None),) * 6,
        check_vma=False,
    )
```

time: 344 us -> 175 us (0.51)
  waiting for transfers between devices: 272 us -> 0 us
  Pallas kernels: 0 us -> 162 us
  local copies, waits for them, and re-layouts: 50.1 us -> 12.1 us
  between operations: 14.2 us -> 0.66 us
  other arithmetic: 7.2 us -> 0 us
    pallas_call x0 -> x1, Pallas kernels: none -> 162 us  [step(): pl.pallas_call(functools.partial(kernel, n, chips, layers), out_shape=[pl...]
    unnamed x8 -> x0, waiting for transfers between devices: 122 us -> none
    all_gather x3 -> x0, waiting for transfers between devices: 121 us -> none  [step(): whole = [lax.all_gather(one[0], 'dp', axis=1, tiled=True) for one in new]]
    unnamed x27 -> x9, local copies, waits for them, and re-layouts: 50.1 us -> 12.1 us
    reduce_scatter x1 -> x0, waiting for transfers between devices: 28.5 us -> none  [step(): lax.psum_scatter(t[0], 'dp', scatter_dimension=1, tiled=True)]
    convert_element_type x3 -> x0, other arithmetic: 7.2 us -> none  [adamw(): return ((w - 0.02 * step).astype(jnp.bfloat16), m, v)]
  transfers between devices with their start and end apart: 6 -> 0, of which waited for: 6 -> 0; matrix products, arithmetic and copies ran while one was open for 14% -> 0% of each run, Pallas kernels for 0% -> 0%
where the time goes in v1:
time: 175 us
  Pallas kernels  162 us (93%)
  local copies, waits for them, and re-layouts  12.1 us (7%)
    pallas_call x1, Pallas kernels, step(): pl.pallas_call(functools.partial(kernel, n, chips, layers), out_shape=[pl...  162 us
    unnamed x9, local copies, waits for them, and re-layouts  12.1 us

profile of v1, /device:TPU:21, one launch (start us, length us, event | category | flops | bytes accessed | tf_op | source)
XLA Modules:
  0.0 175.2 jit_solution(4752943196351448481)
XLA Ops:
  0.6 162.5 %step.1 = (bf16[2,8,2,5,8,2048]{5,4,3,2,1,0:T(8,128)(2,1)S(1)}, bf16[2,8,2,5,8,2048]{5,4,3,2,1,0:T(8,128)(2,1)S(1)}, bf16[2,8,2,16,8,640]{5,4,3,2,1,0:T(8,128)(2...) custom-call(bf16[2,8,2,5,8,2048]{5,4,3,2,1,0:T(8,128)(2,1)} %bitcast, ...), custom_call_target="tpu_custom_call" | custom-call | tf_op jit(solution)/shard_map/step/pallas_call | solution.py:167
  163.1 2.4 %copy.30 = bf16[2,640,2048]{2,1,0:T(8,128)(2,1)} copy(bf16[2,640,2048]{2,1,0:T(8,128)(2,1)S(1)} %bitcast.23) | data formatting | bytes 10485760
  165.5 2.4 %copy.31 = bf16[2,640,2048]{2,1,0:T(8,128)(2,1)} copy(bf16[2,640,2048]{2,1,0:T(8,128)(2,1)S(1)} %bitcast.22) | data formatting | bytes 10485760
  167.9 0.8 copy.33
  168.7 0.8 copy.34
  169.5 0.8 copy.35
  170.4 0.8 copy.36
  171.2 0.8 copy.37
  172.0 0.8 copy.38
  172.9 2.4 %copy.32 = bf16[2,2048,640]{2,1,0:T(8,128)(2,1)} copy(bf16[2,2048,640]{2,1,0:T(8,128)(2,1)S(1)} %bitcast.21) | data formatting | bytes 10485760

commit v2 on v1

--- a/solution.py
+++ b/solution.py
@@ -24,8 +24,8 @@
     take = lambda count: [next(refs) for _ in range(count)]
     g, w, m_in, v_in = take(n), take(n), take(n), take(n)
     new_w, new_m, new_v = take(n), take(n), take(n)
-    own, pair, ring, old_w = take(n), take(n), take(n), take(n)
-    (load_sem, state_sem, pair_recv, ring_recv, gather_recv, share_recv, pair_send, ring_send, gather_send, share_send) = take(10)
+    own, pair, ring, stage, old_w = take(n), take(n), take(n), take(n), take(n)
+    (load_sem, stage_sem, state_sem, pair_recv, ring_recv, gather_recv, share_recv, stage_send, pair_send, ring_send, gather_send, share_send) = take(12)
 
     me = lax.axis_index("dp")
     chip, core = me // CORES, me % CORES
@@ -46,6 +46,14 @@
     def load(a, step, layer):
         return pltpu.make_async_copy(g[a].at[layer, block(step, layer), core], own[a].at[step, layer], load_sem.at[a, step, layer])
 
+    def prepare(a, layer):
+        return pltpu.make_async_copy(g[a].at[layer, block(0, layer), other], stage[a].at[layer], stage_sem.at[a, layer])
+
+    def first_swap(a, layer):
+        return pltpu.make_async_remote_copy(
+            stage[a].at[layer], pair[a].at[0, layer], stage_send.at[a], pair_recv.at[a, 0, layer], partner, MESH
+        )
+
     def swap(a, step, layer):
         return pltpu.make_async_remote_copy(
             g[a].at[layer, block(step, layer), other], pair[a].at[step, layer], pair_send.at[a], pair_recv.at[a, step, layer], partner, MESH
@@ -70,24 +78,27 @@
             pltpu.make_async_copy(v_in[a], new_v[a], state_sem.at[1, a]),
         ] + [pltpu.make_async_copy(w[a].at[layer, chip, core], old_w[a].at[layer], state_sem.at[2 + layer, a]) for layer in range(layers)]
 
-    @pl.loop(0, chips)
-    def _(step):
-        for a, layer in pieces:
-            load(a, step, layer).start()
-
     barrier = pltpu.get_barrier_semaphore()
     for device in (partner, right, left):
         pl.semaphore_signal(barrier, inc=1, device_id=device, device_id_type=MESH)
+    for a, layer in pieces:
+        prepare(a, layer).start()
+        load(a, 0, layer).start()
+
+    @pl.loop(1, chips)
+    def _(step):
+        for a, layer in pieces:
+            load(a, step, layer).start()
+
     pl.semaphore_wait(barrier, 3)
-
-    @pl.loop(0, chips)
+    for a, layer in pieces:
+        prepare(a, layer).wait()
+        first_swap(a, layer).start()
+
+    @pl.loop(1, chips)
     def _(step):
         for a, layer in pieces:
             swap(a, step, layer).start()
-
-    for a in range(n):
-        for copy in states(a):
-            copy.start()
 
     def total(a, step, layer, i, arrived):
         t = own[a][step, layer, i].astype(jnp.float32) + pair[a][step, layer, i].astype(jnp.float32)
@@ -109,6 +120,9 @@
             hop(a, step, layer).start()
 
     pair_sum(0, None)
+    for a in range(n):
+        for copy in states(a):
+            copy.start()
 
     @pl.loop(1, chips - 1)
     def _(step):
@@ -144,10 +158,24 @@
         share(a, last, layer).start()
 
     for a in range(n):
-        pltpu.make_async_remote_copy(pair[a], pair[a], pair_send.at[a], share_recv.at[a], partner, MESH).wait_send()
+        pltpu.make_async_remote_copy(stage[a], stage[a], stage_send.at[a], share_recv.at[a], partner, MESH).wait_send()
+        pltpu.make_async_remote_copy(ring[a], ring[a], pair_send.at[a], share_recv.at[a], partner, MESH).wait_send()
         pltpu.make_async_remote_copy(ring[a], ring[a], ring_send.at[a], share_recv.at[a], partner, MESH).wait_send()
         pltpu.make_async_remote_copy(ring[a], ring[a], gather_send.at[a], share_recv.at[a], partner, MESH).wait_send()
         pltpu.make_async_remote_copy(pair[a], pair[a], share_send.at[a], share_recv.at[a], partner, MESH).wait()
+
+
+def write(count, *refs):
+    sources, targets, sem = refs[:count], refs[count:-1], refs[-1]
+    copies = [
+        pltpu.make_async_copy(source.at[i], target.at[i], sem.at[k, i])
+        for k, (source, target) in enumerate(zip(sources, targets, strict=True))
+        for i in range(source.shape[0])
+    ]
+    for copy in copies:
+        copy.start()
+    for copy in copies:
+        copy.wait()
 
 
 def solution(mesh):
@@ -174,20 +202,27 @@
                 *vmem((chips, layers), jnp.bfloat16),
                 *vmem((chips - 1, layers), jnp.bfloat16),
                 *vmem((layers,), jnp.bfloat16),
+                *vmem((layers,), jnp.bfloat16),
                 sems(n, chips, layers),
+                sems(n, layers),
                 sems(2 + layers, n),
                 sems(n, chips, layers),
                 sems(n, chips - 1, layers),
                 sems(n, chips - 1, layers),
-                sems(n),
-                sems(n),
-                sems(n),
-                sems(n),
-                sems(n),
+                *[sems(n)] * 6,
             ],
             compiler_params=pltpu.CompilerParams(collective_id=0, has_side_effects=True, vmem_limit_bytes=40 << 20),
             name="step",
         )(*operands)
+        out = pl.pallas_call(
+            functools.partial(write, len(out)),
+            out_shape=[jax.ShapeDtypeStruct(one.shape, one.dtype) for one in out],
+            in_specs=[pl.BlockSpec(memory_space=pltpu.VMEM)] * len(out),
+            out_specs=[pl.BlockSpec(memory_space=pl.ANY)] * len(out),
+            scratch_shapes=[sems(len(out), layers)],
+            compiler_params=pltpu.CompilerParams(vmem_limit_bytes=1 << 20),
+            name="write",
+        )(*[pltpu.with_memory_space_constraint(one, pltpu.VMEM) for one in out])
         return tuple(one.reshape(like.shape) for one, like in zip(out, (*weights, *m, *v), strict=True))
 
     all_of, cut = P(None, None, None), P(None, "dp", None)

time: 175 us -> 170 us (0.971)
  local copies, waits for them, and re-layouts: 12.1 us -> 0 us
  Pallas kernels: 162 us -> 169 us
    unnamed x9 -> x0, local copies, waits for them, and re-layouts: 12.1 us -> none
    pallas_call x0 -> x1, Pallas kernels: none -> 6.85 us  [step(): pl.pallas_call(functools.partial(write, len(out)), out_shape=[jax.ShapeDt...]
where the time goes in v2:
time: 170 us
  Pallas kernels  169 us (99%)
    pallas_call x1, Pallas kernels, step(): pl.pallas_call(functools.partial(kernel, n, chips, layers), out_shape=[pl...  163 us
    pallas_call x1, Pallas kernels, step(): pl.pallas_call(functools.partial(write, len(out)), out_shape=[jax.ShapeDt...  6.85 us

profile of v2, /device:TPU:21, one launch (start us, length us, event | category | flops | bytes accessed | tf_op | source)
XLA Modules:
  0.0 170.1 jit_solution(90857686379705333)
XLA Ops:
  0.6 162.6 %step.1 = (bf16[2,8,2,5,8,2048]{5,4,3,2,1,0:T(8,128)(2,1)S(1)}, bf16[2,8,2,5,8,2048]{5,4,3,2,1,0:T(8,128)(2,1)S(1)}, bf16[2,8,2,16,8,640]{5,4,3,2,1,0:T(8,128)(2...) custom-call(bf16[2,8,2,5,8,2048]{5,4,3,2,1,0:T(8,128)(2,1)} %bitcast, ...), custom_call_target="tpu_custom_call" | custom-call | tf_op jit(solution)/shard_map/step/pallas_call | solution.py:195
  163.2 6.9 %write.1 = (bf16[2,8,2,5,8,2048]{5,4,3,2,1,0:T(8,128)(2,1)}, bf16[2,8,2,5,8,2048]{5,4,3,2,1,0:T(8,128)(2,1)}, bf16[2,8,2,16,8,640]{5,4,3,2,1,0:T(8,128)(2,1)}, f...) custom-call(bf16[2,8,2,5,8,2048]{5,4,3,2,1,0:T(8,128)(2,1)S(1)} %get, ...), custom_call_target="tpu_custom_call" | custom-call | tf_op jit(solution)/shard_map/write/pallas_call | solution.py:217

commit v3 on v2

v3 whole, which is shorter than its diff:
```python
import functools

import jax
import jax.numpy as jnp
from jax import lax
from jax.experimental import pallas as pl
from jax.experimental.pallas import tpu as pltpu
from jax.sharding import PartitionSpec as P

MESH = pl.DeviceIdType.MESH
CORES = 2
SUBLANES = 8


def adamw(w, m, v, g):
    m = 0.9 * m + 0.1 * g
    v = 0.95 * v + 0.05 * g * g
    step = m * lax.rsqrt(v + 1e-8) + 0.1 * w
    return (w - 0.02 * step).astype(jnp.bfloat16), m, v


def kernel(n, chips, layers, *refs):
    refs = iter(refs)
    take = lambda count: [next(refs) for _ in range(count)]
    g, w, m_in, v_in = take(n), take(n), take(n), take(n)
    new_w, new_m, new_v = take(n), take(n), take(n)
    own, pair, ring, stage, old_w = take(n), take(n), take(n), take(n), take(n)
    load_sem, stage_sem, state_sem, first_recv, pair_recv, ring_recv, share_recv, swap_send, ring_send = take(9)

    me = lax.axis_index("dp")
    chip, core = me // CORES, me % CORES
    other = 1 - core
    last = chips - 1
    partner = {"dp": chip * CORES + other}
    to = [1 - 2 * ((layer + core) % 2) for layer in range(layers)]
    ahead = [{"dp": (chip + chips + d) % chips * CORES + core} for d in to]
    pieces = [(a, layer) for a in range(n) for layer in range(layers)]

    def block(step, way):
        return (chip + 2 * chips - way * (step + 1)) % chips

    def source(step, layer):
        return (chip + chips - to[layer] * step) % chips

    def load(a, step, layer):
        return pltpu.make_async_copy(g[a].at[layer, block(step, to[layer]), core], own[a].at[step, layer], load_sem.at[a, step % 2])

    def prepare(a, layer):
        return pltpu.make_async_copy(g[a].at[layer, block(0, -to[layer]), other], stage[a].at[layer], stage_sem.at[a])

    def first_swap(a, layer):
        return pltpu.make_async_remote_copy(
            stage[a].at[layer], pair[a].at[0, layer], swap_send.at[a], first_recv.at[a, layer], partner, MESH
        )

    def swap(a, step, layer):
        return pltpu.make_async_remote_copy(
            g[a].at[layer, block(step, -to[layer]), other], pair[a].at[step, layer], swap_send.at[a], pair_recv.at[a, step - 1], partner, MESH
        )

    def hop(a, step, layer):
        return pltpu.make_async_remote_copy(
            own[a].at[step, layer], ring[a].at[step, layer], ring_send.at[a], ring_recv.at[a, step, layer], ahead[layer], MESH
        )

    def spread(a, step, layer):
        here = new_w[a].at[layer, source(step, layer), core]
        return pltpu.make_async_remote_copy(
            here, here, ring_send.at[a], ring_recv.at[a, (step + last) % chips, layer], ahead[layer], MESH
        )

    def share(a, step, layer):
        here = new_w[a].at[layer, source(step, layer), core]
        return pltpu.make_async_remote_copy(here, here, swap_send.at[a], share_recv.at[a], partner, MESH)

    def wait_both(here, sem):
        pltpu.make_async_copy(here, here, sem).wait()

    def take_own(a, step):
        wait_both(own[a].at[step], load_sem.at[a, step % 2])

    def take_pair(a, step):
        wait_both(pair[a].at[step], pair_recv.at[a, step - 1])

    def fetch(step):
        for a, layer in pieces:
            swap(a, step, layer).start()
        for a, layer in pieces:
            load(a, step, layer).start()

    barrier = pltpu.get_barrier_semaphore()
    for device in (*(dict(dp=(chip + d) % chips * CORES + core) for d in (1, last)), partner):
        pl.semaphore_signal(barrier, inc=1, device_id=device, device_id_type=MESH)
    for a, layer in pieces:
        prepare(a, layer).start()
    for a, layer in pieces:
        load(a, 0, layer).start()
    pl.semaphore_wait(barrier, 3)
    for a in range(n):
        wait_both(stage[a], stage_sem.at[a])
        for layer in range(layers):
            first_swap(a, layer).start()
    fetch(1)

    def total(a, step, layer, i, arrived):
        t = own[a][step, layer, i].astype(jnp.float32) + pair[a][step, layer, i].astype(jnp.float32)
        if arrived is not None:
            t = t + ring[a][arrived, layer, i].astype(jnp.float32)
        return t

    def pass_on(a, step, layer, arrived):
        @pl.loop(0, own[a].shape[2])
        def _(i):
            own[a][step, layer, i] = total(a, step, layer, i, arrived).astype(jnp.bfloat16)

        hop(a, step, layer).start()

    for a, layer in pieces:
        if layer == 0:
            take_own(a, 0)
        first_swap(a, layer).wait_recv()
        pass_on(a, 0, layer, None)

    for a in range(n):
        pltpu.make_async_copy(m_in[a], new_m[a], state_sem.at[0, a]).start()
        pltpu.make_async_copy(v_in[a], new_v[a], state_sem.at[1, a]).start()
        for layer in range(layers):
            pltpu.make_async_copy(w[a].at[layer, chip, core], old_w[a].at[layer], state_sem.at[2, a]).start()

    @pl.loop(1, last)
    def _(step):
        fetch(step + 1)
        for a, layer in pieces:
            if layer == 0:
                take_own(a, step)
                take_pair(a, step)
            hop(a, step - 1, layer).wait_recv()
            pass_on(a, step, layer, step - 1)

    for a in range(n):
        wait_both(new_m[a], state_sem.at[0, a])
        wait_both(new_v[a], state_sem.at[1, a])
        wait_both(old_w[a], state_sem.at[2, a])
    for a, layer in pieces:
        if layer == 0:
            take_own(a, last)
            take_pair(a, last)
        hop(a, last - 1, layer).wait_recv()

        @pl.loop(0, own[a].shape[2])
        def _(i):
            grad = total(a, last, layer, i, last - 1).astype(jnp.bfloat16).astype(jnp.float32)
            new = adamw(old_w[a][layer, i].astype(jnp.float32), new_m[a][layer, i], new_v[a][layer, i], grad)
            new_w[a][layer, chip, core, i], new_m[a][layer, i], new_v[a][layer, i] = new

        spread(a, 0, layer).start()
        share(a, 0, layer).start()

    @pl.loop(1, last)
    def _(step):
        for a, layer in pieces:
            spread(a, step - 1, layer).wait_recv()
            spread(a, step, layer).start()
            share(a, step, layer).start()

    for a, layer in pieces:
        spread(a, last - 1, layer).wait_recv()
        share(a, last, layer).start()

    for a in range(n):
        wait_both(new_w[a], swap_send.at[a])
        wait_both(new_w[a].at[:, pl.ds(0, last)], ring_send.at[a])
    for a in range(n):
        wait_both(pair[a], share_recv.at[a])


def write(count, *refs):
    sources, targets, sem = refs[:count], refs[count:-1], refs[-1]
    copies = [pltpu.make_async_copy(source, target, sem.at[k]) for k, (source, target) in enumerate(zip(sources, targets, strict=True))]
    for copy in copies:
        copy.start()
    for copy in copies:
        copy.wait()


def solution(mesh):
    chips = mesh.shape["dp"] // CORES

    def step(*arrays):
        terms, weights, m, v = (arrays[i : i + 3] for i in (0, 3, 6, 9))
        n, layers = len(terms), weights[0].shape[0]
        tiles = [(one.shape[1] // SUBLANES, SUBLANES, one.shape[2]) for one in m]
        whole = [(layers, chips, CORES, *tile) for tile in tiles]
        state = [(layers, *tile) for tile in tiles]
        operands = [one.reshape(shape) for one, shape in zip(terms, whole, strict=True)]
        operands += [one.reshape(shape) for one, shape in zip(weights, whole, strict=True)]
        operands += [one.reshape(shape) for part in (m, v) for one, shape in zip(part, state, strict=True)]
        sems = lambda *shape: pltpu.SemaphoreType.DMA(shape)
        vmem = lambda lead, dtype: [pltpu.VMEM((*lead, *tile), dtype) for tile in tiles]
        out = pl.pallas_call(
            functools.partial(kernel, n, chips, layers),
            out_shape=[pltpu.VMEM(shape, jnp.bfloat16) for shape in whole] + [pltpu.VMEM(shape, jnp.float32) for shape in state] * 2,
            in_specs=[pl.BlockSpec(memory_space=pl.ANY)] * len(operands),
            out_specs=[pl.BlockSpec(memory_space=pltpu.VMEM)] * (3 * n),
            scratch_shapes=[
                *vmem((chips, layers), jnp.bfloat16),
                *vmem((chips, layers), jnp.bfloat16),
                *vmem((chips - 1, layers), jnp.bfloat16),
                *vmem((layers,), jnp.bfloat16),
                *vmem((layers,), jnp.bfloat16),
                sems(n, 2),
                sems(n),
                sems(3, n),
                sems(n, layers),
                sems(n, chips - 1),
                sems(n, chips, layers),
                sems(n),
                sems(n),
                sems(n),
            ],
            compiler_params=pltpu.CompilerParams(collective_id=0, has_side_effects=True, vmem_limit_bytes=40 << 20),
            name="step",
        )(*operands)
        out = pl.pallas_call(
            functools.partial(write, len(out)),
            out_shape=[jax.ShapeDtypeStruct(one.shape, one.dtype) for one in out],
            in_specs=[pl.BlockSpec(memory_space=pltpu.VMEM)] * len(out),
            out_specs=[pl.BlockSpec(memory_space=pl.ANY)] * len(out),
            scratch_shapes=[sems(len(out))],
            compiler_params=pltpu.CompilerParams(vmem_limit_bytes=1 << 20),
            name="write",
        )(*[pltpu.with_memory_space_constraint(one, pltpu.VMEM) for one in out])
        return tuple(one.reshape(like.shape) for one, like in zip(out, (*weights, *m, *v), strict=True))

    all_of, cut = P(None, None, None), P(None, "dp", None)
    return jax.shard_map(
        step,
        mesh=mesh,
        in_specs=(P(("rep", "dp"), None, None, None),) * 3 + (all_of,) * 3 + (cut,) * 6,
        out_specs=(P("rep", None, None),) * 3 + (P("rep", "dp", None),) * 6,
        check_vma=False,
    )
```

time: 170 us -> 169 us (level)
  no operation moved by 1% of the time
where the time goes in v3:
time: 169 us
  Pallas kernels  168 us (99%)
    pallas_call x1, Pallas kernels, step(): pl.pallas_call(functools.partial(kernel, n, chips, layers), out_shape=[pl...  162 us
    pallas_call x1, Pallas kernels, step(): pl.pallas_call(functools.partial(write, len(out)), out_shape=[jax.ShapeDt...  6.79 us

profile of v3, /device:TPU:21, one launch (start us, length us, event | category | flops | bytes accessed | tf_op | source)
XLA Modules:
  0.0 169.1 jit_solution(4294928742808089337)
XLA Ops:
  0.6 161.7 %step.1 = (bf16[2,8,2,5,8,2048]{5,4,3,2,1,0:T(8,128)(2,1)S(1)}, bf16[2,8,2,5,8,2048]{5,4,3,2,1,0:T(8,128)(2,1)S(1)}, bf16[2,8,2,16,8,640]{5,4,3,2,1,0:T(8,128)(2...) custom-call(bf16[2,8,2,5,8,2048]{5,4,3,2,1,0:T(8,128)(2,1)} %bitcast, ...), custom_call_target="tpu_custom_call" | custom-call | tf_op jit(solution)/shard_map/step/pallas_call | solution.py:200
  162.3 6.8 %write.1 = (bf16[2,8,2,5,8,2048]{5,4,3,2,1,0:T(8,128)(2,1)}, bf16[2,8,2,5,8,2048]{5,4,3,2,1,0:T(8,128)(2,1)}, bf16[2,8,2,16,8,640]{5,4,3,2,1,0:T(8,128)(2,1)}, f...) custom-call(bf16[2,8,2,5,8,2048]{5,4,3,2,1,0:T(8,128)(2,1)S(1)} %get, ...), custom_call_target="tpu_custom_call" | custom-call | tf_op jit(solution)/shard_map/write/pallas_call | solution.py:224

commit v4 on v3

v4 whole, which is shorter than its diff:
```python
import functools

import jax
import jax.numpy as jnp
from jax import lax
from jax.experimental import pallas as pl
from jax.experimental.pallas import tpu as pltpu
from jax.sharding import PartitionSpec as P

MESH = pl.DeviceIdType.MESH
CORES = 2
SUBLANES = 8
HEAD = 1
PARTS = 4
DETOUR = 0
SLOTS = 3


def adamw(w, m, v, g):
    m = 0.9 * m + 0.1 * g
    v = 0.95 * v + 0.05 * g * g
    step = m * lax.rsqrt(v + 1e-8) + 0.1 * w
    return (w - 0.02 * step).astype(jnp.bfloat16), m, v


def cuts(count, parts):
    edges = [count * i // parts for i in range(parts + 1)]
    return [(lo, hi - lo) for lo, hi in zip(edges, edges[1:])]


def kernel(n, chips, layers, *refs):
    refs = iter(refs)
    take = lambda count: [next(refs) for _ in range(count)]
    g, w, m_in, v_in = take(n), take(n), take(n), take(n)
    new_w, new_m, new_v = take(n), take(n), take(n)
    own, pair, ring, stage, old_w = take(n), take(n), take(n), take(n), take(n)
    stage_sem, first_load, load_sem, first_recv, pair_recv, ring_recv, tail_recv, detour_recv, share_recv, swap_send, ring_send, credit = take(12)

    me = lax.axis_index("dp")
    chip, core = me // CORES, me % CORES
    other = 1 - core
    last = chips - 1
    partner = {"dp": chip * CORES + other}
    right = {"dp": (chip + 1) % chips * CORES + core}
    left = {"dp": (chip + last) % chips * CORES + core}
    ahead = [left if layer % 2 else right for layer in range(layers)]
    behind = [right if layer % 2 else left for layer in range(layers)]
    slabs = [one.shape[2] for one in own]
    pieces = [(a, layer) for a in range(n) for layer in range(layers)]
    units = [(0, 0, HEAD), (0, HEAD, slabs[0] - HEAD)] + [(a, 0, slabs[a]) for a in range(1, n)]

    def block(step, layer):
        return (chip + 1 + step if layer % 2 else chip + chips - 1 - step) % chips

    def source(step, layer):
        return (chip + step if layer % 2 else chip + chips - step) % chips

    def prepare(u, layer):
        a, lo, size = units[u]
        return pltpu.make_async_copy(
            g[a].at[layer, block(0, layer), other, pl.ds(lo, size)], stage[a].at[layer, pl.ds(lo, size)], stage_sem.at[u]
        )

    def first_own(u, layer):
        a, lo, size = units[u]
        return pltpu.make_async_copy(
            g[a].at[layer, block(0, layer), core, pl.ds(lo, size)], own[a].at[0, layer, pl.ds(lo, size)], first_load.at[u]
        )

    def first_swap(u, layer):
        a, lo, size = units[u]
        return pltpu.make_async_remote_copy(
            stage[a].at[layer, pl.ds(lo, size)], pair[a].at[0, layer, pl.ds(lo, size)], swap_send.at[a], first_recv.at[u, layer], partner, MESH
        )

    def load(a, step, layer):
        return pltpu.make_async_copy(g[a].at[layer, block(step, layer), core], own[a].at[step, layer], load_sem.at[a])

    def swap(a, step, layer, sem):
        return pltpu.make_async_remote_copy(
            g[a].at[layer, block(step, layer), other], pair[a].at[step, layer], swap_send.at[a], pair_recv.at[sem, a], partner, MESH
        )

    def hop(a, step, layer, lo=0, size=None):
        part = pl.ds(lo, slabs[a] if size is None else size)
        return pltpu.make_async_remote_copy(
            own[a].at[step, layer, part],
            ring[a].at[step, layer, part],
            ring_send.at[a],
            ring_recv.at[a, step % SLOTS, layer],
            ahead[layer],
            MESH,
        )

    def spread(a, step, layer):
        here = new_w[a].at[layer, source(step, layer), core]
        return pltpu.make_async_remote_copy(
            here, here, ring_send.at[a], ring_recv.at[a, (step + last) % SLOTS, layer], ahead[layer], MESH
        )

    def tail(layer):
        return cuts(slabs[n - 1] - (0 if layer % 2 else DETOUR), PARTS)

    def spread_tail(step, layer, k):
        here = new_w[n - 1].at[layer, source(step, layer), core, pl.ds(*tail(layer)[k])]
        return pltpu.make_async_remote_copy(here, here, ring_send.at[n - 1], tail_recv.at[k, layer], ahead[layer], MESH)

    def detour(step, layer):
        here = new_w[n - 1].at[layer, source(step, layer), core, pl.ds(slabs[n - 1] - DETOUR, DETOUR)]
        return pltpu.make_async_remote_copy(here, here, ring_send.at[n - 1], detour_recv.at[layer], behind[layer], MESH)

    def share(a, step, layer, lo=0, size=None):
        here = new_w[a].at[layer, source(step, layer), core, pl.ds(lo, slabs[a] if size is None else size)]
        return pltpu.make_async_remote_copy(here, here, swap_send.at[a], share_recv.at[a], partner, MESH)

    def wait_all(here, sem):
        pltpu.make_async_copy(here, here, sem).wait()

    def grant(layer):
        pl.semaphore_signal(credit.at[layer], inc=1, device_id=behind[layer], device_id_type=MESH)

    def spend(layer):
        pl.semaphore_wait(credit.at[layer], 1)

    for layer in range(layers):
        prepare(0, layer).start()
    for layer in range(layers):
        first_own(0, layer).start()
    barrier = pltpu.get_barrier_semaphore()
    for device in (right, left, partner):
        pl.semaphore_signal(barrier, inc=1, device_id=device, device_id_type=MESH)
    for u in range(1, n + 1):
        for layer in range(layers):
            prepare(u, layer).start()
    pl.semaphore_wait(barrier, 3)
    for u, (a, lo, size) in enumerate(units):
        wait_all(stage[a].at[:, pl.ds(lo, size)], stage_sem.at[u])
        for layer in range(layers):
            first_swap(u, layer).start()
        if u:
            for layer in range(layers):
                first_own(u, layer).start()
    for a, layer in pieces:
        swap(a, 1, layer, 0).start()

    def total(a, step, layer, i, arrived):
        t = own[a][step, layer, i].astype(jnp.float32) + pair[a][step, layer, i].astype(jnp.float32)
        if arrived is not None:
            t = t + ring[a][arrived, layer, i].astype(jnp.float32)
        return t

    def pass_on(a, step, layer, arrived, lo, size):
        @pl.loop(lo, lo + size)
        def _(i):
            own[a][step, layer, i] = total(a, step, layer, i, arrived).astype(jnp.bfloat16)

        hop(a, step, layer, lo, size).start()

    for u, (a, lo, size) in enumerate(units):
        wait_all(own[a].at[0, :, pl.ds(lo, size)], first_load.at[u])
        for layer in range(layers):
            first_swap(u, layer).wait_recv()
            pass_on(a, 0, layer, None, lo, size)

    @pl.loop(1, chips)
    def _(step):
        for a, layer in pieces:
            load(a, step, layer).start()

    @pl.loop(2, chips)
    def _(step):
        for a, layer in pieces:
            swap(a, step, layer, 1).start()

    for a in range(n):
        pltpu.make_async_copy(m_in[a], new_m[a], load_sem.at[a]).start()
        pltpu.make_async_copy(v_in[a], new_v[a], load_sem.at[a]).start()
        for layer in range(layers):
            pltpu.make_async_copy(w[a].at[layer, chip, core], old_w[a].at[layer], load_sem.at[a]).start()
    for a in range(n):
        wait_all(new_w[a].at[:, pl.ds(0, (last + 1 + 4) // CORES)], load_sem.at[a])
        wait_all(pair[a].at[1], pair_recv.at[0, a])

    @pl.loop(1, last)
    def _(step):
        @pl.when(step == 2)
        def _():
            for a in range(n):
                wait_all(pair[a].at[pl.ds(2, chips - 2)], pair_recv.at[1, a])

        @pl.when(step >= SLOTS)
        def _():
            for layer in range(layers):
                spend(layer)

        for a, layer in pieces:
            hop(a, step - 1, layer).wait_recv()
            pass_on(a, step, layer, step - 1, 0, slabs[a])
            if a == n - 1:
                grant(layer)

    for layer in range(layers):
        spend(layer)
    for a, layer in pieces:
        hop(a, last - 1, layer).wait_recv()

        @pl.loop(0, slabs[a])
        def _(i):
            grad = total(a, last, layer, i, last - 1).astype(jnp.bfloat16).astype(jnp.float32)
            new = adamw(old_w[a][layer, i].astype(jnp.float32), new_m[a][layer, i], new_v[a][layer, i], grad)
            new_w[a][layer, chip, core, i], new_m[a][layer, i], new_v[a][layer, i] = new

        spread(a, 0, layer).start()
        share(a, 0, layer).start()
        if a == n - 1:
            grant(layer)
            if DETOUR and layer % 2 == 0:
                detour(0, layer).start()

    @pl.loop(1, last - 1)
    def _(step):
        for layer in range(layers):
            spend(layer)
        for a, layer in pieces:
            spread(a, step - 1, layer).wait_recv()
            spread(a, step, layer).start()
            share(a, step, layer).start()
            if a == n - 1:

                @pl.when(step <= last - SLOTS)
                def _():
                    grant(layer)

    for layer in range(layers):
        spend(layer)
        if DETOUR and layer % 2 == 0:
            detour(0, layer).wait_recv()
            share(n - 1, last, layer, slabs[n - 1] - DETOUR, DETOUR).start()
    for a, layer in pieces:
        spread(a, last - 2, layer).wait_recv()
        if a < n - 1:
            spread(a, last - 1, layer).start()
        else:
            for k in range(PARTS):
                spread_tail(last - 1, layer, k).start()
        share(a, last - 1, layer).start()

    for a in range(n - 1):
        for layer in range(layers):
            spread(a, last - 1, layer).wait_recv()
            share(a, last, layer).start()
    for k in range(PARTS):
        for layer in range(layers):
            spread_tail(last, layer, k).wait_recv()
            share(n - 1, last, layer, *tail(layer)[k]).start()

    for a in range(n):
        wait_all(new_w[a], swap_send.at[a])
        wait_all(new_w[a].at[:, pl.ds(0, last)], ring_send.at[a])
    for a in range(n):
        wait_all(pair[a], share_recv.at[a])


def write(count, *refs):
    sources, targets, sem = refs[:count], refs[count:-1], refs[-1]
    copies = [pltpu.make_async_copy(source, target, sem.at[k]) for k, (source, target) in enumerate(zip(sources, targets, strict=True))]
    for copy in copies:
        copy.start()
    for copy in copies:
        copy.wait()


def solution(mesh):
    chips = mesh.shape["dp"] // CORES

    def step(*arrays):
        terms, weights, m, v = (arrays[i : i + 3] for i in (0, 3, 6, 9))
        n, layers = len(terms), weights[0].shape[0]
        tiles = [(one.shape[1] // SUBLANES, SUBLANES, one.shape[2]) for one in m]
        whole = [(layers, chips, CORES, *tile) for tile in tiles]
        state = [(layers, *tile) for tile in tiles]
        operands = [one.reshape(shape) for one, shape in zip(terms, whole, strict=True)]
        operands += [one.reshape(shape) for one, shape in zip(weights, whole, strict=True)]
        operands += [one.reshape(shape) for part in (m, v) for one, shape in zip(part, state, strict=True)]
        sems = lambda *shape: pltpu.SemaphoreType.DMA(shape)
        vmem = lambda lead, dtype: [pltpu.VMEM((*lead, *tile), dtype) for tile in tiles]
        out = pl.pallas_call(
            functools.partial(kernel, n, chips, layers),
            out_shape=[pltpu.VMEM(shape, jnp.bfloat16) for shape in whole] + [pltpu.VMEM(shape, jnp.float32) for shape in state] * 2,
            in_specs=[pl.BlockSpec(memory_space=pl.ANY)] * len(operands),
            out_specs=[pl.BlockSpec(memory_space=pltpu.VMEM)] * (3 * n),
            scratch_shapes=[
                *vmem((chips, layers), jnp.bfloat16),
                *vmem((chips, layers), jnp.bfloat16),
                *vmem((chips - 1, layers), jnp.bfloat16),
                *vmem((layers,), jnp.bfloat16),
                *vmem((layers,), jnp.bfloat16),
                sems(n + 1),
                sems(n + 1),
                sems(n),
                sems(n + 1, layers),
                sems(2, n),
                sems(n, SLOTS, layers),
                sems(PARTS, layers),
                sems(layers),
                sems(n),
                sems(n),
                sems(n),
                pltpu.SemaphoreType.REGULAR((layers,)),
            ],
            compiler_params=pltpu.CompilerParams(collective_id=0, has_side_effects=True, vmem_limit_bytes=40 << 20),
            name="step",
        )(*operands)
        out = pl.pallas_call(
            functools.partial(write, len(out)),
            out_shape=[jax.ShapeDtypeStruct(one.shape, one.dtype) for one in out],
            in_specs=[pl.BlockSpec(memory_space=pltpu.VMEM)] * len(out),
            out_specs=[pl.BlockSpec(memory_space=pl.ANY)] * len(out),
            scratch_shapes=[sems(len(out))],
            compiler_params=pltpu.CompilerParams(vmem_limit_bytes=1 << 20),
            name="write",
        )(*[pltpu.with_memory_space_constraint(one, pltpu.VMEM) for one in out])
        return tuple(one.reshape(like.shape) for one, like in zip(out, (*weights, *m, *v), strict=True))

    all_of, cut = P(None, None, None), P(None, "dp", None)
    return jax.shard_map(
        step,
        mesh=mesh,
        in_specs=(P(("rep", "dp"), None, None, None),) * 3 + (all_of,) * 3 + (cut,) * 6,
        out_specs=(P("rep", None, None),) * 3 + (P("rep", "dp", None),) * 6,
        check_vma=False,
    )
```

time: 169 us -> 168 us (level)
  no operation moved by 1% of the time
where the time goes in v4:
time: 168 us
  Pallas kernels  167 us (99%)
    pallas_call x1, Pallas kernels, step(): pl.pallas_call(functools.partial(kernel, n, chips, layers), out_shape=[pl...  160 us
    pallas_call x1, Pallas kernels, step(): pl.pallas_call(functools.partial(write, len(out)), out_shape=[jax.ShapeDt...  6.79 us

profile of v4, /device:TPU:21, one launch (start us, length us, event | category | flops | bytes accessed | tf_op | source)
XLA Modules:
  0.0 167.9 jit_solution(16298639561593883592)
XLA Ops:
  0.6 160.5 %step.1 = (bf16[2,8,2,5,8,2048]{5,4,3,2,1,0:T(8,128)(2,1)S(1)}, bf16[2,8,2,5,8,2048]{5,4,3,2,1,0:T(8,128)(2,1)S(1)}, bf16[2,8,2,16,8,640]{5,4,3,2,1,0:T(8,128)(2...) custom-call(bf16[2,8,2,5,8,2048]{5,4,3,2,1,0:T(8,128)(2,1)} %bitcast, ...), custom_call_target="tpu_custom_call" | custom-call | tf_op jit(solution)/shard_map/step/pallas_call | solution.py:287
  161.1 6.8 %write.1 = (bf16[2,8,2,5,8,2048]{5,4,3,2,1,0:T(8,128)(2,1)}, bf16[2,8,2,5,8,2048]{5,4,3,2,1,0:T(8,128)(2,1)}, bf16[2,8,2,16,8,640]{5,4,3,2,1,0:T(8,128)(2,1)}, f...) custom-call(bf16[2,8,2,5,8,2048]{5,4,3,2,1,0:T(8,128)(2,1)S(1)} %get, ...), custom_call_target="tpu_custom_call" | custom-call | tf_op jit(solution)/shard_map/write/pallas_call | solution.py:314

commit v5 on v4

--- a/solution.py
+++ b/solution.py
@@ -12,7 +12,7 @@
 SUBLANES = 8
 HEAD = 1
 PARTS = 4
-DETOUR = 0
+DETOUR = 6
 SLOTS = 3
 
 
@@ -261,13 +261,18 @@
         wait_all(pair[a], share_recv.at[a])
 
 
-def write(count, *refs):
-    sources, targets, sem = refs[:count], refs[count:-1], refs[-1]
-    copies = [pltpu.make_async_copy(source, target, sem.at[k]) for k, (source, target) in enumerate(zip(sources, targets, strict=True))]
+def write(n, *refs):
+    *refs, sem = refs
+    sources, targets = refs[: 3 * n], refs[3 * n :]
+    copies = [
+        pltpu.make_async_copy(source, target, sem.at[min(k, n)]) for k, (source, target) in enumerate(zip(sources, targets, strict=True))
+    ]
     for copy in copies:
         copy.start()
-    for copy in copies:
+    for copy in copies[:n]:
         copy.wait()
+    part = sources[0].at[:, pl.ds(0, 2 * n)]
+    pltpu.make_async_copy(part, part, sem.at[n]).wait()
 
 
 def solution(mesh):
@@ -312,11 +317,11 @@
             name="step",
         )(*operands)
         out = pl.pallas_call(
-            functools.partial(write, len(out)),
+            functools.partial(write, n),
             out_shape=[jax.ShapeDtypeStruct(one.shape, one.dtype) for one in out],
             in_specs=[pl.BlockSpec(memory_space=pltpu.VMEM)] * len(out),
             out_specs=[pl.BlockSpec(memory_space=pl.ANY)] * len(out),
-            scratch_shapes=[sems(len(out))],
+            scratch_shapes=[sems(n + 1)],
             compiler_params=pltpu.CompilerParams(vmem_limit_bytes=1 << 20),
             name="write",
         )(*[pltpu.with_memory_space_constraint(one, pltpu.VMEM) for one in out])

time: 168 us -> 167 us (level)
  no operation moved by 1% of the time
where the time goes in v5:
time: 167 us
  Pallas kernels  166 us (99%)
    pallas_call x1, Pallas kernels, step(): pl.pallas_call(functools.partial(kernel, n, chips, layers), out_shape=[pl...  159 us
    pallas_call x1, Pallas kernels, step(): pl.pallas_call(functools.partial(write, n), out_shape=[jax.ShapeDtypeStru...  6.74 us

profile of v5, /device:TPU:21, one launch (start us, length us, event | category | flops | bytes accessed | tf_op | source)
XLA Modules:
  0.0 166.6 jit_solution(12092526939545699411)
XLA Ops:
  0.6 159.2 %step.1 = (bf16[2,8,2,5,8,2048]{5,4,3,2,1,0:T(8,128)(2,1)S(1)}, bf16[2,8,2,5,8,2048]{5,4,3,2,1,0:T(8,128)(2,1)S(1)}, bf16[2,8,2,16,8,640]{5,4,3,2,1,0:T(8,128)(2...) custom-call(bf16[2,8,2,5,8,2048]{5,4,3,2,1,0:T(8,128)(2,1)} %bitcast, ...), custom_call_target="tpu_custom_call" | custom-call | tf_op jit(solution)/shard_map/step/pallas_call | solution.py:292
  159.8 6.7 %write.1 = (bf16[2,8,2,5,8,2048]{5,4,3,2,1,0:T(8,128)(2,1)}, bf16[2,8,2,5,8,2048]{5,4,3,2,1,0:T(8,128)(2,1)}, bf16[2,8,2,16,8,640]{5,4,3,2,1,0:T(8,128)(2,1)}, f...) custom-call(bf16[2,8,2,5,8,2048]{5,4,3,2,1,0:T(8,128)(2,1)S(1)} %get, ...), custom_call_target="tpu_custom_call" | custom-call | tf_op jit(solution)/shard_map/write/pallas_call | solution.py:319

commit v6 on v5

--- a/solution.py
+++ b/solution.py
@@ -12,7 +12,7 @@
 SUBLANES = 8
 HEAD = 1
 PARTS = 4
-DETOUR = 6
+DETOUR = 10
 SLOTS = 3
 
 
@@ -34,7 +34,7 @@
     g, w, m_in, v_in = take(n), take(n), take(n), take(n)
     new_w, new_m, new_v = take(n), take(n), take(n)
     own, pair, ring, stage, old_w = take(n), take(n), take(n), take(n), take(n)
-    stage_sem, first_load, load_sem, first_recv, pair_recv, ring_recv, tail_recv, detour_recv, share_recv, swap_send, ring_send, credit = take(12)
+    stage_sem, first_load, load_sem, first_recv, pair_recv, ring_recv, tail_recv, detour_recv, share_recv, swap_send, ring_send, credit, entered = take(13)
 
     me = lax.axis_index("dp")
     chip, core = me // CORES, me % CORES
@@ -127,12 +127,40 @@
     for layer in range(layers):
         first_own(0, layer).start()
     barrier = pltpu.get_barrier_semaphore()
-    for device in (right, left, partner):
+
+    def greet(device):
         pl.semaphore_signal(barrier, inc=1, device_id=device, device_id_type=MESH)
+
+    def answer(which, device):
+        pl.semaphore_signal(entered.at[which], inc=1, device_id=device, device_id_type=MESH)
+
+    def answer_chips():
+        @pl.when(chip > 0)
+        def _():
+            answer(0, left)
+
+        @pl.when(chip == last)
+        def _():
+            answer(1, right)
+
+    greeted = jnp.where(chip > 0, 1, 0) + jnp.where(chip == last, 1, 0)
+    pl.when(chip < last)(lambda: greet(right))
+    pl.when(chip == 0)(lambda: greet(left))
+    pl.when(core == 0)(lambda: greet(partner))
     for u in range(1, n + 1):
         for layer in range(layers):
             prepare(u, layer).start()
-    pl.semaphore_wait(barrier, 3)
+
+    @pl.when(core > 0)
+    def _():
+        pl.semaphore_wait(barrier, greeted + 1)
+        answer(2, partner)
+        answer_chips()
+
+    @pl.when(core == 0)
+    def _():
+        pl.semaphore_wait(entered.at[2], 1)
+
     for u, (a, lo, size) in enumerate(units):
         wait_all(stage[a].at[:, pl.ds(lo, size)], stage_sem.at[u])
         for layer in range(layers):
@@ -143,24 +171,38 @@
     for a, layer in pieces:
         swap(a, 1, layer, 0).start()
 
+    @pl.when(core == 0)
+    def _():
+        @pl.when(chip > 0)
+        def _():
+            pl.semaphore_wait(barrier, greeted)
+
+        answer_chips()
+
     def total(a, step, layer, i, arrived):
         t = own[a][step, layer, i].astype(jnp.float32) + pair[a][step, layer, i].astype(jnp.float32)
         if arrived is not None:
             t = t + ring[a][arrived, layer, i].astype(jnp.float32)
         return t
 
-    def pass_on(a, step, layer, arrived, lo, size):
+    def add(a, step, layer, arrived, lo, size):
         @pl.loop(lo, lo + size)
         def _(i):
             own[a][step, layer, i] = total(a, step, layer, i, arrived).astype(jnp.bfloat16)
 
-        hop(a, step, layer, lo, size).start()
-
     for u, (a, lo, size) in enumerate(units):
         wait_all(own[a].at[0, :, pl.ds(lo, size)], first_load.at[u])
         for layer in range(layers):
             first_swap(u, layer).wait_recv()
-            pass_on(a, 0, layer, None, lo, size)
+            add(a, 0, layer, None, lo, size)
+        for layer in reversed(range(layers)):
+            if u == 0 and layer < 2:
+
+                @pl.when(chip == 0 if layer else chip < last)
+                def _():
+                    pl.semaphore_wait(entered.at[layer], 1)
+
+            hop(a, 0, layer, lo, size).start()
 
     @pl.loop(1, chips)
     def _(step):
@@ -195,7 +237,8 @@
 
         for a, layer in pieces:
             hop(a, step - 1, layer).wait_recv()
-            pass_on(a, step, layer, step - 1, 0, slabs[a])
+            add(a, step, layer, step - 1, 0, slabs[a])
+            hop(a, step, layer).start()
             if a == n - 1:
                 grant(layer)
 
@@ -312,6 +355,7 @@
                 sems(n),
                 sems(n),
                 pltpu.SemaphoreType.REGULAR((layers,)),
+                pltpu.SemaphoreType.REGULAR((3,)),
             ],
             compiler_params=pltpu.CompilerParams(collective_id=0, has_side_effects=True, vmem_limit_bytes=40 << 20),
             name="step",

time: 167 us -> 166 us (level)
  no operation moved by 1% of the time
where the time goes in v6:
time: 166 us
  Pallas kernels  165 us (99%)
    pallas_call x1, Pallas kernels, step(): pl.pallas_call(functools.partial(kernel, n, chips, layers), out_shape=[pl...  158 us
    pallas_call x1, Pallas kernels, step(): pl.pallas_call(functools.partial(write, n), out_shape=[jax.ShapeDtypeStru...  6.74 us

profile of v6, /device:TPU:21, one launch (start us, length us, event | category | flops | bytes accessed | tf_op | source)
XLA Modules:
  0.0 165.7 jit_solution(2261519115933501421)
XLA Ops:
  0.6 158.3 %step.1 = (bf16[2,8,2,5,8,2048]{5,4,3,2,1,0:T(8,128)(2,1)S(1)}, bf16[2,8,2,5,8,2048]{5,4,3,2,1,0:T(8,128)(2,1)S(1)}, bf16[2,8,2,16,8,640]{5,4,3,2,1,0:T(8,128)(2...) custom-call(bf16[2,8,2,5,8,2048]{5,4,3,2,1,0:T(8,128)(2,1)} %bitcast, ...), custom_call_target="tpu_custom_call" | custom-call | tf_op jit(solution)/shard_map/step/pallas_call | solution.py:335
  159.0 6.7 %write.1 = (bf16[2,8,2,5,8,2048]{5,4,3,2,1,0:T(8,128)(2,1)}, bf16[2,8,2,5,8,2048]{5,4,3,2,1,0:T(8,128)(2,1)}, bf16[2,8,2,16,8,640]{5,4,3,2,1,0:T(8,128)(2,1)}, f...) custom-call(bf16[2,8,2,5,8,2048]{5,4,3,2,1,0:T(8,128)(2,1)S(1)} %get, ...), custom_call_target="tpu_custom_call" | custom-call | tf_op jit(solution)/shard_map/write/pallas_call | solution.py:363

commit v7 on v6

--- a/solution.py
+++ b/solution.py
@@ -12,7 +12,8 @@
 SUBLANES = 8
 HEAD = 1
 PARTS = 4
-DETOUR = 10
+SEAM = 13
+DETOUR = 5
 SLOTS = 3
 
 
@@ -33,8 +34,8 @@
     take = lambda count: [next(refs) for _ in range(count)]
     g, w, m_in, v_in = take(n), take(n), take(n), take(n)
     new_w, new_m, new_v = take(n), take(n), take(n)
-    own, pair, ring, stage, old_w = take(n), take(n), take(n), take(n), take(n)
-    stage_sem, first_load, load_sem, first_recv, pair_recv, ring_recv, tail_recv, detour_recv, share_recv, swap_send, ring_send, credit, entered = take(13)
+    own, pair, ring, stage, old_w, (extra,) = take(n), take(n), take(n), take(n), take(n), take(1)
+    stage_sem, first_load, load_sem, first_recv, pair_recv, ring_recv, tail_recv, extra_recv, share_recv, swap_send, ring_send, gather_send, tail_send, credit, entered = take(15)
 
     me = lax.axis_index("dp")
     chip, core = me // CORES, me % CORES
@@ -46,6 +47,8 @@
     ahead = [left if layer % 2 else right for layer in range(layers)]
     behind = [right if layer % 2 else left for layer in range(layers)]
     slabs = [one.shape[2] for one in own]
+    end = n - 1
+    whole, split = slabs[end], slabs[end] - SEAM
     pieces = [(a, layer) for a in range(n) for layer in range(layers)]
     units = [(0, 0, HEAD), (0, HEAD, slabs[0] - HEAD)] + [(a, 0, slabs[a]) for a in range(1, n)]
 
@@ -95,19 +98,22 @@
     def spread(a, step, layer):
         here = new_w[a].at[layer, source(step, layer), core]
         return pltpu.make_async_remote_copy(
-            here, here, ring_send.at[a], ring_recv.at[a, (step + last) % SLOTS, layer], ahead[layer], MESH
-        )
-
-    def tail(layer):
-        return cuts(slabs[n - 1] - (0 if layer % 2 else DETOUR), PARTS)
+            here, here, gather_send.at[a], ring_recv.at[a, (step + last) % SLOTS, layer], ahead[layer], MESH
+        )
+
+    def straight():
+        return pltpu.make_async_remote_copy(own[end].at[0, 0, pl.ds(split, SEAM)], extra, ring_send.at[end], extra_recv, left, MESH)
+
+    tail = [cuts(whole, PARTS) if layer else [(whole - DETOUR, DETOUR), *cuts(whole - DETOUR, PARTS)] for layer in range(layers)]
 
     def spread_tail(step, layer, k):
-        here = new_w[n - 1].at[layer, source(step, layer), core, pl.ds(*tail(layer)[k])]
-        return pltpu.make_async_remote_copy(here, here, ring_send.at[n - 1], tail_recv.at[k, layer], ahead[layer], MESH)
-
-    def detour(step, layer):
-        here = new_w[n - 1].at[layer, source(step, layer), core, pl.ds(slabs[n - 1] - DETOUR, DETOUR)]
-        return pltpu.make_async_remote_copy(here, here, ring_send.at[n - 1], detour_recv.at[layer], behind[layer], MESH)
+        here = new_w[end].at[layer, source(step, layer), core, pl.ds(*tail[layer][k])]
+        sem = tail_send.at[layers if layer == k == 0 else layer]
+        return pltpu.make_async_remote_copy(here, here, sem, tail_recv.at[k, layer], ahead[layer], MESH)
+
+    def detour(step):
+        here = new_w[end].at[0, source(step, 0), core, pl.ds(*tail[0][0])]
+        return pltpu.make_async_remote_copy(here, here, tail_send.at[layers + 1], tail_recv.at[0, 0], left, MESH)
 
     def share(a, step, layer, lo=0, size=None):
         here = new_w[a].at[layer, source(step, layer), core, pl.ds(lo, slabs[a] if size is None else size)]
@@ -195,14 +201,35 @@
         for layer in range(layers):
             first_swap(u, layer).wait_recv()
             add(a, 0, layer, None, lo, size)
-        for layer in reversed(range(layers)):
-            if u == 0 and layer < 2:
-
-                @pl.when(chip == 0 if layer else chip < last)
-                def _():
-                    pl.semaphore_wait(entered.at[layer], 1)
-
-            hop(a, 0, layer, lo, size).start()
+
+        @pl.when(chip > 0)
+        def _():
+            hop(a, 0, 1, lo, size).start()
+
+        if u == 0:
+
+            @pl.when(chip < last)
+            def _():
+                pl.semaphore_wait(entered.at[0], 1)
+
+        if a < end:
+            hop(a, 0, 0, lo, size).start()
+        else:
+            hop(a, 0, 0, 0, split).start()
+
+            @pl.when(chip < last)
+            def _():
+                hop(a, 0, 0, split, SEAM).start()
+
+            @pl.when(chip == last)
+            def _():
+                straight().start()
+
+    @pl.when(chip == 0)
+    def _():
+        pl.semaphore_wait(entered.at[1], 1)
+        for a, lo, size in units:
+            hop(a, 0, 1, lo, size).start()
 
     @pl.loop(1, chips)
     def _(step):
@@ -236,29 +263,65 @@
                 spend(layer)
 
         for a, layer in pieces:
-            hop(a, step - 1, layer).wait_recv()
-            add(a, step, layer, step - 1, 0, slabs[a])
+            if (a, layer) == (end, 0):
+                short = (step == 1) & (chip == 0)
+
+                @pl.when(short)
+                def _():
+                    hop(a, 0, layer, 0, split).wait_recv()
+                    add(a, step, layer, None, split, SEAM)
+
+                @pl.when(jnp.logical_not(short))
+                def _():
+                    hop(a, step - 1, layer).wait_recv()
+                    add(a, step, layer, step - 1, split, SEAM)
+
+                add(a, step, layer, step - 1, 0, split)
+            else:
+                hop(a, step - 1, layer).wait_recv()
+                add(a, step, layer, step - 1, 0, slabs[a])
             hop(a, step, layer).start()
-            if a == n - 1:
+            if a == end:
                 grant(layer)
+
+    def update(a, layer, lo, size, more=None):
+        @pl.loop(lo, lo + size)
+        def _(i):
+            grad = total(a, last, layer, i, last - 1)
+            if more is not None:
+                grad = grad + more(i)
+            grad = grad.astype(jnp.bfloat16).astype(jnp.float32)
+            new = adamw(old_w[a][layer, i].astype(jnp.float32), new_m[a][layer, i], new_v[a][layer, i], grad)
+            new_w[a][layer, chip, core, i], new_m[a][layer, i], new_v[a][layer, i] = new
 
     for layer in range(layers):
         spend(layer)
     for a, layer in pieces:
         hop(a, last - 1, layer).wait_recv()
 
-        @pl.loop(0, slabs[a])
-        def _(i):
-            grad = total(a, last, layer, i, last - 1).astype(jnp.bfloat16).astype(jnp.float32)
-            new = adamw(old_w[a][layer, i].astype(jnp.float32), new_m[a][layer, i], new_v[a][layer, i], grad)
-            new_w[a][layer, chip, core, i], new_m[a][layer, i], new_v[a][layer, i] = new
-
+        if (a, layer) == (end, 0):
+            update(a, layer, 0, split)
+
+            @pl.when(chip == last - 1)
+            def _():
+                straight().wait_recv()
+                update(a, layer, split, SEAM, lambda i: extra[i - split].astype(jnp.float32))
+
+            @pl.when(chip != last - 1)
+            def _():
+                update(a, layer, split, SEAM)
+
+        else:
+            update(a, layer, 0, slabs[a])
         spread(a, 0, layer).start()
         share(a, 0, layer).start()
-        if a == n - 1:
+        if a == end:
             grant(layer)
-            if DETOUR and layer % 2 == 0:
-                detour(0, layer).start()
+            if layer == 0:
+
+                @pl.when(chip == 1)
+                def _():
+                    detour(0).start()
 
     @pl.loop(1, last - 1)
     def _(step):
@@ -268,7 +331,7 @@
             spread(a, step - 1, layer).wait_recv()
             spread(a, step, layer).start()
             share(a, step, layer).start()
-            if a == n - 1:
+            if a == end:
 
                 @pl.when(step <= last - SLOTS)
                 def _():
@@ -276,30 +339,46 @@
 
     for layer in range(layers):
         spend(layer)
-        if DETOUR and layer % 2 == 0:
-            detour(0, layer).wait_recv()
-            share(n - 1, last, layer, slabs[n - 1] - DETOUR, DETOUR).start()
     for a, layer in pieces:
         spread(a, last - 2, layer).wait_recv()
-        if a < n - 1:
+        if a < end:
             spread(a, last - 1, layer).start()
         else:
-            for k in range(PARTS):
+            if layer == 0:
+
+                @pl.when(chip < last)
+                def _():
+                    spread_tail(last - 1, 0, 0).start()
+
+            for k in range(1 - layer, len(tail[layer])):
                 spread_tail(last - 1, layer, k).start()
         share(a, last - 1, layer).start()
 
-    for a in range(n - 1):
+    for a in range(end):
         for layer in range(layers):
             spread(a, last - 1, layer).wait_recv()
             share(a, last, layer).start()
-    for k in range(PARTS):
-        for layer in range(layers):
-            spread_tail(last, layer, k).wait_recv()
-            share(n - 1, last, layer, *tail(layer)[k]).start()
-
+    for k in range(PARTS + 1):
+        for layer in range(layers):
+            if k < len(tail[layer]):
+                spread_tail(last, layer, k).wait_recv()
+                share(end, last, layer, *tail[layer][k]).start()
+
+    @pl.when(chip < last)
+    def _():
+        spread_tail(last - 1, 0, 0).wait_send()
+
+    @pl.when(chip == 1)
+    def _():
+        detour(0).wait_send()
+
+    for layer in range(layers):
+        lo, size = 0, whole - (0 if layer else DETOUR)
+        wait_all(new_w[end].at[layer, 0, 0, pl.ds(lo, size)], tail_send.at[layer])
     for a in range(n):
         wait_all(new_w[a], swap_send.at[a])
-        wait_all(new_w[a].at[:, pl.ds(0, last)], ring_send.at[a])
+        wait_all(ring[a], ring_send.at[a])
+        wait_all(ring[a] if a < end else ring[a].at[pl.ds(0, last - 1)], gather_send.at[a])
     for a in range(n):
         wait_all(pair[a], share_recv.at[a])
 
@@ -343,17 +422,20 @@
                 *vmem((chips - 1, layers), jnp.bfloat16),
                 *vmem((layers,), jnp.bfloat16),
                 *vmem((layers,), jnp.bfloat16),
+                pltpu.VMEM((SEAM, *tiles[-1][1:]), jnp.bfloat16),
                 sems(n + 1),
                 sems(n + 1),
                 sems(n),
                 sems(n + 1, layers),
                 sems(2, n),
                 sems(n, SLOTS, layers),
-                sems(PARTS, layers),
-                sems(layers),
+                sems(PARTS + 1, layers),
+                pltpu.SemaphoreType.DMA,
                 sems(n),
                 sems(n),
                 sems(n),
+                sems(n),
+                sems(layers + 2),
                 pltpu.SemaphoreType.REGULAR((layers,)),
                 pltpu.SemaphoreType.REGULAR((3,)),
             ],

time: 166 us -> 164 us (0.988)
  Pallas kernels: 165 us -> 163 us
where the time goes in v7:
time: 164 us
  Pallas kernels  163 us (99%)
    pallas_call x1, Pallas kernels, step(): pl.pallas_call(functools.partial(kernel, n, chips, layers), out_shape=[pl...  157 us
    pallas_call x1, Pallas kernels, step(): pl.pallas_call(functools.partial(write, n), out_shape=[jax.ShapeDtypeStru...  6.74 us

profile of v7, /device:TPU:21, one launch (start us, length us, event | category | flops | bytes accessed | tf_op | source)
XLA Modules:
  0.0 164.2 jit_solution(788651831829657587)
XLA Ops:
  0.6 156.8 %step.1 = (bf16[2,8,2,5,8,2048]{5,4,3,2,1,0:T(8,128)(2,1)S(1)}, bf16[2,8,2,5,8,2048]{5,4,3,2,1,0:T(8,128)(2,1)S(1)}, bf16[2,8,2,16,8,640]{5,4,3,2,1,0:T(8,128)(2...) custom-call(bf16[2,8,2,5,8,2048]{5,4,3,2,1,0:T(8,128)(2,1)} %bitcast, ...), custom_call_target="tpu_custom_call" | custom-call | tf_op jit(solution)/shard_map/step/pallas_call | solution.py:414
  157.4 6.7 %write.1 = (bf16[2,8,2,5,8,2048]{5,4,3,2,1,0:T(8,128)(2,1)}, bf16[2,8,2,5,8,2048]{5,4,3,2,1,0:T(8,128)(2,1)}, bf16[2,8,2,16,8,640]{5,4,3,2,1,0:T(8,128)(2,1)}, f...) custom-call(bf16[2,8,2,5,8,2048]{5,4,3,2,1,0:T(8,128)(2,1)S(1)} %get, ...), custom_call_target="tpu_custom_call" | custom-call | tf_op jit(solution)/shard_map/write/pallas_call | solution.py:445

commit v8 on v7

--- a/solution.py
+++ b/solution.py
@@ -12,8 +12,9 @@
 SUBLANES = 8
 HEAD = 1
 PARTS = 4
-SEAM = 13
-DETOUR = 5
+SEAM = 10
+LIFT = 9
+DETOUR = 10
 SLOTS = 3
 
 
@@ -34,7 +35,7 @@
     take = lambda count: [next(refs) for _ in range(count)]
     g, w, m_in, v_in = take(n), take(n), take(n), take(n)
     new_w, new_m, new_v = take(n), take(n), take(n)
-    own, pair, ring, stage, old_w, (extra,) = take(n), take(n), take(n), take(n), take(n), take(1)
+    own, pair, ring, stage, old_w, extra = take(n), take(n), take(n), take(n), take(n), take(2)
     stage_sem, first_load, load_sem, first_recv, pair_recv, ring_recv, tail_recv, extra_recv, share_recv, swap_send, ring_send, gather_send, tail_send, credit, entered = take(15)
 
     me = lax.axis_index("dp")
@@ -48,7 +49,9 @@
     behind = [right if layer % 2 else left for layer in range(layers)]
     slabs = [one.shape[2] for one in own]
     end = n - 1
-    whole, split = slabs[end], slabs[end] - SEAM
+    whole = slabs[end]
+    giver, taker = (last, 1), (last - 1, 2)
+    split = [whole - SEAM, whole - LIFT]
     pieces = [(a, layer) for a in range(n) for layer in range(layers)]
     units = [(0, 0, HEAD), (0, HEAD, slabs[0] - HEAD)] + [(a, 0, slabs[a]) for a in range(1, n)]
 
@@ -101,8 +104,11 @@
             here, here, gather_send.at[a], ring_recv.at[a, (step + last) % SLOTS, layer], ahead[layer], MESH
         )
 
-    def straight():
-        return pltpu.make_async_remote_copy(own[end].at[0, 0, pl.ds(split, SEAM)], extra, ring_send.at[end], extra_recv, left, MESH)
+    def straight(layer):
+        part = pl.ds(split[layer], whole - split[layer])
+        return pltpu.make_async_remote_copy(
+            own[end].at[0, layer, part], extra[layer], ring_send.at[end], extra_recv.at[layer], behind[layer], MESH
+        )
 
     tail = [cuts(whole, PARTS) if layer else [(whole - DETOUR, DETOUR), *cuts(whole - DETOUR, PARTS)] for layer in range(layers)]
 
@@ -202,9 +208,23 @@
             first_swap(u, layer).wait_recv()
             add(a, 0, layer, None, lo, size)
 
+        def send(layer):
+            if a < end:
+                hop(a, 0, layer, lo, size).start()
+                return
+            hop(a, 0, layer, 0, split[layer]).start()
+
+            @pl.when(chip != giver[layer])
+            def _():
+                hop(a, 0, layer, split[layer], whole - split[layer]).start()
+
+            @pl.when(chip == giver[layer])
+            def _():
+                straight(layer).start()
+
         @pl.when(chip > 0)
         def _():
-            hop(a, 0, 1, lo, size).start()
+            send(1)
 
         if u == 0:
 
@@ -212,18 +232,7 @@
             def _():
                 pl.semaphore_wait(entered.at[0], 1)
 
-        if a < end:
-            hop(a, 0, 0, lo, size).start()
-        else:
-            hop(a, 0, 0, 0, split).start()
-
-            @pl.when(chip < last)
-            def _():
-                hop(a, 0, 0, split, SEAM).start()
-
-            @pl.when(chip == last)
-            def _():
-                straight().start()
+        send(0)
 
     @pl.when(chip == 0)
     def _():
@@ -263,20 +272,21 @@
                 spend(layer)
 
         for a, layer in pieces:
-            if (a, layer) == (end, 0):
+            if a == end:
                 short = (step == 1) & (chip == 0)
+                cut = split[layer]
 
                 @pl.when(short)
                 def _():
-                    hop(a, 0, layer, 0, split).wait_recv()
-                    add(a, step, layer, None, split, SEAM)
+                    hop(a, 0, layer, 0, cut).wait_recv()
+                    add(a, step, layer, None, cut, whole - cut)
 
                 @pl.when(jnp.logical_not(short))
                 def _():
                     hop(a, step - 1, layer).wait_recv()
-                    add(a, step, layer, step - 1, split, SEAM)
-
-                add(a, step, layer, step - 1, 0, split)
+                    add(a, step, layer, step - 1, cut, whole - cut)
+
+                add(a, step, layer, step - 1, 0, cut)
             else:
                 hop(a, step - 1, layer).wait_recv()
                 add(a, step, layer, step - 1, 0, slabs[a])
@@ -299,17 +309,18 @@
     for a, layer in pieces:
         hop(a, last - 1, layer).wait_recv()
 
-        if (a, layer) == (end, 0):
-            update(a, layer, 0, split)
-
-            @pl.when(chip == last - 1)
+        if a == end:
+            cut = split[layer]
+            update(a, layer, 0, cut)
+
+            @pl.when(chip == taker[layer])
             def _():
-                straight().wait_recv()
-                update(a, layer, split, SEAM, lambda i: extra[i - split].astype(jnp.float32))
-
-            @pl.when(chip != last - 1)
+                straight(layer).wait_recv()
+                update(a, layer, cut, whole - cut, lambda i: extra[layer][i - cut].astype(jnp.float32))
+
+            @pl.when(chip != taker[layer])
             def _():
-                update(a, layer, split, SEAM)
+                update(a, layer, cut, whole - cut)
 
         else:
             update(a, layer, 0, slabs[a])
@@ -422,7 +433,7 @@
                 *vmem((chips - 1, layers), jnp.bfloat16),
                 *vmem((layers,), jnp.bfloat16),
                 *vmem((layers,), jnp.bfloat16),
-                pltpu.VMEM((SEAM, *tiles[-1][1:]), jnp.bfloat16),
+                *[pltpu.VMEM((slabs, *tiles[-1][1:]), jnp.bfloat16) for slabs in (SEAM, LIFT)],
                 sems(n + 1),
                 sems(n + 1),
                 sems(n),
@@ -430,7 +441,7 @@
                 sems(2, n),
                 sems(n, SLOTS, layers),
                 sems(PARTS + 1, layers),
-                pltpu.SemaphoreType.DMA,
+                sems(layers),
                 sems(n),
                 sems(n),
                 sems(n),

time: 164 us -> 164 us (level)
  no operation moved by 1% of the time
where the time goes in v8:
time: 164 us
  Pallas kernels  163 us (99%)
    pallas_call x1, Pallas kernels, step(): pl.pallas_call(functools.partial(kernel, n, chips, layers), out_shape=[pl...  156 us
    pallas_call x1, Pallas kernels, step(): pl.pallas_call(functools.partial(write, n), out_shape=[jax.ShapeDtypeStru...  6.74 us

profile of v8, /device:TPU:21, one launch (start us, length us, event | category | flops | bytes accessed | tf_op | source)
XLA Modules:
  0.0 163.5 jit_solution(8550545558025739156)
XLA Ops:
  0.6 156.1 %step.1 = (bf16[2,8,2,5,8,2048]{5,4,3,2,1,0:T(8,128)(2,1)S(1)}, bf16[2,8,2,5,8,2048]{5,4,3,2,1,0:T(8,128)(2,1)S(1)}, bf16[2,8,2,16,8,640]{5,4,3,2,1,0:T(8,128)(2...) custom-call(bf16[2,8,2,5,8,2048]{5,4,3,2,1,0:T(8,128)(2,1)} %bitcast, ...), custom_call_target="tpu_custom_call" | custom-call | tf_op jit(solution)/shard_map/step/pallas_call | solution.py:425
  156.8 6.7 %write.1 = (bf16[2,8,2,5,8,2048]{5,4,3,2,1,0:T(8,128)(2,1)}, bf16[2,8,2,5,8,2048]{5,4,3,2,1,0:T(8,128)(2,1)}, bf16[2,8,2,16,8,640]{5,4,3,2,1,0:T(8,128)(2,1)}, f...) custom-call(bf16[2,8,2,5,8,2048]{5,4,3,2,1,0:T(8,128)(2,1)S(1)} %get, ...), custom_call_target="tpu_custom_call" | custom-call | tf_op jit(solution)/shard_map/write/pallas_call | solution.py:456

commit v9 on v8

--- a/solution.py
+++ b/solution.py
@@ -11,7 +11,7 @@
 CORES = 2
 SUBLANES = 8
 HEAD = 1
-PARTS = 4
+PARTS = 2
 SEAM = 10
 LIFT = 9
 DETOUR = 10
@@ -76,7 +76,7 @@
     def first_swap(u, layer):
         a, lo, size = units[u]
         return pltpu.make_async_remote_copy(
-            stage[a].at[layer, pl.ds(lo, size)], pair[a].at[0, layer, pl.ds(lo, size)], swap_send.at[a], first_recv.at[u, layer], partner, MESH
+            stage[a].at[layer, pl.ds(lo, size)], pair[a].at[0, layer, pl.ds(lo, size)], swap_send.at[a], first_recv.at[u], partner, MESH
         )
 
     def load(a, step, layer):
@@ -101,7 +101,7 @@
     def spread(a, step, layer):
         here = new_w[a].at[layer, source(step, layer), core]
         return pltpu.make_async_remote_copy(
-            here, here, gather_send.at[a], ring_recv.at[a, (step + last) % SLOTS, layer], ahead[layer], MESH
+            here, here, ring_send.at[a] if a < end else gather_send, ring_recv.at[a, (step + last) % SLOTS, layer], ahead[layer], MESH
         )
 
     def straight(layer):
@@ -204,8 +204,8 @@
 
     for u, (a, lo, size) in enumerate(units):
         wait_all(own[a].at[0, :, pl.ds(lo, size)], first_load.at[u])
-        for layer in range(layers):
-            first_swap(u, layer).wait_recv()
+        wait_all(pair[a].at[0, :, pl.ds(lo, size)], first_recv.at[u])
+        for layer in range(layers):
             add(a, 0, layer, None, lo, size)
 
         def send(layer):
@@ -388,8 +388,8 @@
         wait_all(new_w[end].at[layer, 0, 0, pl.ds(lo, size)], tail_send.at[layer])
     for a in range(n):
         wait_all(new_w[a], swap_send.at[a])
-        wait_all(ring[a], ring_send.at[a])
-        wait_all(ring[a] if a < end else ring[a].at[pl.ds(0, last - 1)], gather_send.at[a])
+        wait_all(new_w[a].at[:, pl.ds(0, last)] if a < end else ring[a], ring_send.at[a])
+    wait_all(ring[end].at[pl.ds(0, last - 1)], gather_send)
     for a in range(n):
         wait_all(pair[a], share_recv.at[a])
 
@@ -397,13 +397,15 @@
 def write(n, *refs):
     *refs, sem = refs
     sources, targets = refs[: 3 * n], refs[3 * n :]
-    copies = [
-        pltpu.make_async_copy(source, target, sem.at[min(k, n)]) for k, (source, target) in enumerate(zip(sources, targets, strict=True))
-    ]
-    for copy in copies:
-        copy.start()
-    for copy in copies[:n]:
-        copy.wait()
+    weights = list(zip(sources, targets, strict=True))[:n]
+    for a, (source, target) in enumerate(weights):
+        for layer in range(source.shape[0]):
+            for chip in range(source.shape[1]):
+                pltpu.make_async_copy(source.at[layer, chip], target.at[layer, chip], sem.at[a]).start()
+    for source, target in zip(sources[n:], targets[n:], strict=True):
+        pltpu.make_async_copy(source, target, sem.at[n]).start()
+    for a, (source, target) in enumerate(weights):
+        pltpu.make_async_copy(source, target, sem.at[a]).wait()
     part = sources[0].at[:, pl.ds(0, 2 * n)]
     pltpu.make_async_copy(part, part, sem.at[n]).wait()
 
@@ -437,7 +439,7 @@
                 sems(n + 1),
                 sems(n + 1),
                 sems(n),
-                sems(n + 1, layers),
+                sems(n + 1),
                 sems(2, n),
                 sems(n, SLOTS, layers),
                 sems(PARTS + 1, layers),
@@ -445,7 +447,7 @@
                 sems(n),
                 sems(n),
                 sems(n),
-                sems(n),
+                pltpu.SemaphoreType.DMA,
                 sems(layers + 2),
                 pltpu.SemaphoreType.REGULAR((layers,)),
                 pltpu.SemaphoreType.REGULAR((3,)),

time: 164 us -> 164 us (level)
  no operation moved by 1% of the time
where the time goes in v9:
time: 164 us; the launch traced here: 163 us
  Pallas kernels  163 us (99%)
    pallas_call x1, Pallas kernels, step(): pl.pallas_call(functools.partial(kernel, n, chips, layers), out_shape=[pl...  156 us
    pallas_call x1, Pallas kernels, step(): pl.pallas_call(functools.partial(write, n), out_shape=[jax.ShapeDtypeStru...  6.71 us

profile of v9, /device:TPU:21, one launch (start us, length us, event | category | flops | bytes accessed | tf_op | source)
XLA Modules:
  0.0 163.4 jit_solution(15250573302165586403)
XLA Ops:
  0.6 156.1 %step.1 = (bf16[2,8,2,5,8,2048]{5,4,3,2,1,0:T(8,128)(2,1)S(1)}, bf16[2,8,2,5,8,2048]{5,4,3,2,1,0:T(8,128)(2,1)S(1)}, bf16[2,8,2,16,8,640]{5,4,3,2,1,0:T(8,128)(2...) custom-call(bf16[2,8,2,5,8,2048]{5,4,3,2,1,0:T(8,128)(2,1)} %bitcast, ...), custom_call_target="tpu_custom_call" | custom-call | tf_op jit(solution)/shard_map/step/pallas_call | solution.py:427
  156.7 6.7 %write.1 = (bf16[2,8,2,5,8,2048]{5,4,3,2,1,0:T(8,128)(2,1)}, bf16[2,8,2,5,8,2048]{5,4,3,2,1,0:T(8,128)(2,1)}, bf16[2,8,2,16,8,640]{5,4,3,2,1,0:T(8,128)(2,1)}, f...) custom-call(bf16[2,8,2,5,8,2048]{5,4,3,2,1,0:T(8,128)(2,1)S(1)} %get, ...), custom_call_target="tpu_custom_call" | custom-call | tf_op jit(solution)/shard_map/write/pallas_call | solution.py:458

commit v10 on v9

--- a/solution.py
+++ b/solution.py
@@ -13,8 +13,8 @@
 HEAD = 1
 PARTS = 2
 SEAM = 10
-LIFT = 9
-DETOUR = 10
+LIFT = 12
+DETOUR = (12, 4)
 SLOTS = 3
 
 
@@ -110,16 +110,17 @@
             own[end].at[0, layer, part], extra[layer], ring_send.at[end], extra_recv.at[layer], behind[layer], MESH
         )
 
-    tail = [cuts(whole, PARTS) if layer else [(whole - DETOUR, DETOUR), *cuts(whole - DETOUR, PARTS)] for layer in range(layers)]
+    sender, keeper = (1, last - 1), (last, 0)
+    tail = [[(whole - skip, skip), *cuts(whole - skip, PARTS)] for skip in DETOUR]
 
     def spread_tail(step, layer, k):
         here = new_w[end].at[layer, source(step, layer), core, pl.ds(*tail[layer][k])]
-        sem = tail_send.at[layers if layer == k == 0 else layer]
+        sem = tail_send.at[0 if k else 1, layer]
         return pltpu.make_async_remote_copy(here, here, sem, tail_recv.at[k, layer], ahead[layer], MESH)
 
-    def detour(step):
-        here = new_w[end].at[0, source(step, 0), core, pl.ds(*tail[0][0])]
-        return pltpu.make_async_remote_copy(here, here, tail_send.at[layers + 1], tail_recv.at[0, 0], left, MESH)
+    def detour(layer):
+        here = new_w[end].at[layer, chip, core, pl.ds(*tail[layer][0])]
+        return pltpu.make_async_remote_copy(here, here, tail_send.at[2, layer], tail_recv.at[0, layer], behind[layer], MESH)
 
     def share(a, step, layer, lo=0, size=None):
         here = new_w[a].at[layer, source(step, layer), core, pl.ds(lo, slabs[a] if size is None else size)]
@@ -328,11 +329,10 @@
         share(a, 0, layer).start()
         if a == end:
             grant(layer)
-            if layer == 0:
-
-                @pl.when(chip == 1)
-                def _():
-                    detour(0).start()
+
+            @pl.when(chip == sender[layer])
+            def _():
+                detour(layer).start()
 
     @pl.loop(1, last - 1)
     def _(step):
@@ -355,13 +355,12 @@
         if a < end:
             spread(a, last - 1, layer).start()
         else:
-            if layer == 0:
-
-                @pl.when(chip < last)
-                def _():
-                    spread_tail(last - 1, 0, 0).start()
-
-            for k in range(1 - layer, len(tail[layer])):
+
+            @pl.when(chip != keeper[layer])
+            def _():
+                spread_tail(last - 1, layer, 0).start()
+
+            for k in range(1, PARTS + 1):
                 spread_tail(last - 1, layer, k).start()
         share(a, last - 1, layer).start()
 
@@ -371,21 +370,20 @@
             share(a, last, layer).start()
     for k in range(PARTS + 1):
         for layer in range(layers):
-            if k < len(tail[layer]):
-                spread_tail(last, layer, k).wait_recv()
-                share(end, last, layer, *tail[layer][k]).start()
-
-    @pl.when(chip < last)
-    def _():
-        spread_tail(last - 1, 0, 0).wait_send()
-
-    @pl.when(chip == 1)
-    def _():
-        detour(0).wait_send()
+            spread_tail(last, layer, k).wait_recv()
+            share(end, last, layer, *tail[layer][k]).start()
 
     for layer in range(layers):
-        lo, size = 0, whole - (0 if layer else DETOUR)
-        wait_all(new_w[end].at[layer, 0, 0, pl.ds(lo, size)], tail_send.at[layer])
+
+        @pl.when(chip != keeper[layer])
+        def _():
+            spread_tail(last - 1, layer, 0).wait_send()
+
+        @pl.when(chip == sender[layer])
+        def _():
+            detour(layer).wait_send()
+
+        wait_all(new_w[end].at[layer, 0, 0, pl.ds(0, whole - DETOUR[layer])], tail_send.at[0, layer])
     for a in range(n):
         wait_all(new_w[a], swap_send.at[a])
         wait_all(new_w[a].at[:, pl.ds(0, last)] if a < end else ring[a], ring_send.at[a])
@@ -448,7 +446,7 @@
                 sems(n),
                 sems(n),
                 pltpu.SemaphoreType.DMA,
-                sems(layers + 2),
+                sems(3, layers),
                 pltpu.SemaphoreType.REGULAR((layers,)),
                 pltpu.SemaphoreType.REGULAR((3,)),
             ],

time: 164 us -> 163 us (level)
  no operation moved by 1% of the time
where the time goes in v10:
time: 163 us
  Pallas kernels  162 us (99%)
    pallas_call x1, Pallas kernels, step(): pl.pallas_call(functools.partial(kernel, n, chips, layers), out_shape=[pl...  156 us
    pallas_call x1, Pallas kernels, step(): pl.pallas_call(functools.partial(write, n), out_shape=[jax.ShapeDtypeStru...  6.71 us

profile of v10, /device:TPU:21, one launch (start us, length us, event | category | flops | bytes accessed | tf_op | source)
XLA Modules:
  0.0 163.1 jit_solution(13869031763069062852)
XLA Ops:
  0.6 155.8 %step.1 = (bf16[2,8,2,5,8,2048]{5,4,3,2,1,0:T(8,128)(2,1)S(1)}, bf16[2,8,2,5,8,2048]{5,4,3,2,1,0:T(8,128)(2,1)S(1)}, bf16[2,8,2,16,8,640]{5,4,3,2,1,0:T(8,128)(2...) custom-call(bf16[2,8,2,5,8,2048]{5,4,3,2,1,0:T(8,128)(2,1)} %bitcast, ...), custom_call_target="tpu_custom_call" | custom-call | tf_op jit(solution)/shard_map/step/pallas_call | solution.py:425
  156.4 6.7 %write.1 = (bf16[2,8,2,5,8,2048]{5,4,3,2,1,0:T(8,128)(2,1)}, bf16[2,8,2,5,8,2048]{5,4,3,2,1,0:T(8,128)(2,1)}, bf16[2,8,2,16,8,640]{5,4,3,2,1,0:T(8,128)(2,1)}, f...) custom-call(bf16[2,8,2,5,8,2048]{5,4,3,2,1,0:T(8,128)(2,1)S(1)} %get, ...), custom_call_target="tpu_custom_call" | custom-call | tf_op jit(solution)/shard_map/write/pallas_call | solution.py:456

commit v11 on v10

--- a/solution.py
+++ b/solution.py
@@ -15,7 +15,7 @@
 SEAM = 10
 LIFT = 12
 DETOUR = (12, 4)
-SLOTS = 3
+SLOTS = 2
 
 
 def adamw(w, m, v, g):

time: 163 us -> 163 us (level)
  no operation moved by 1% of the time
where the time goes in v11:
time: 163 us
  Pallas kernels  162 us (99%)
    pallas_call x1, Pallas kernels, step(): pl.pallas_call(functools.partial(kernel, n, chips, layers), out_shape=[pl...  156 us
    pallas_call x1, Pallas kernels, step(): pl.pallas_call(functools.partial(write, n), out_shape=[jax.ShapeDtypeStru...  6.71 us

profile of v11, /device:TPU:21, one launch (start us, length us, event | category | flops | bytes accessed | tf_op | source)
XLA Modules:
  0.0 163.1 jit_solution(15427550589916198899)
XLA Ops:
  0.6 155.7 %step.1 = (bf16[2,8,2,5,8,2048]{5,4,3,2,1,0:T(8,128)(2,1)S(1)}, bf16[2,8,2,5,8,2048]{5,4,3,2,1,0:T(8,128)(2,1)S(1)}, bf16[2,8,2,16,8,640]{5,4,3,2,1,0:T(8,128)(2...) custom-call(bf16[2,8,2,5,8,2048]{5,4,3,2,1,0:T(8,128)(2,1)} %bitcast, ...), custom_call_target="tpu_custom_call" | custom-call | tf_op jit(solution)/shard_map/step/pallas_call | solution.py:425
  156.4 6.7 %write.1 = (bf16[2,8,2,5,8,2048]{5,4,3,2,1,0:T(8,128)(2,1)}, bf16[2,8,2,5,8,2048]{5,4,3,2,1,0:T(8,128)(2,1)}, bf16[2,8,2,16,8,640]{5,4,3,2,1,0:T(8,128)(2,1)}, f...) custom-call(bf16[2,8,2,5,8,2048]{5,4,3,2,1,0:T(8,128)(2,1)S(1)} %get, ...), custom_call_target="tpu_custom_call" | custom-call | tf_op jit(solution)/shard_map/write/pallas_call | solution.py:456

commit v12 on v11

--- a/solution.py
+++ b/solution.py
@@ -399,7 +399,8 @@
     for a, (source, target) in enumerate(weights):
         for layer in range(source.shape[0]):
             for chip in range(source.shape[1]):
-                pltpu.make_async_copy(source.at[layer, chip], target.at[layer, chip], sem.at[a]).start()
+                for core in range(source.shape[2]):
+                    pltpu.make_async_copy(source.at[layer, chip, core], target.at[layer, chip, core], sem.at[a]).start()
     for source, target in zip(sources[n:], targets[n:], strict=True):
         pltpu.make_async_copy(source, target, sem.at[n]).start()
     for a, (source, target) in enumerate(weights):

time: 163 us -> 163 us (level)
  no operation moved by 1% of the time
where the time goes in v12:
time: 163 us
  Pallas kernels  162 us (99%)
    pallas_call x1, Pallas kernels, step(): pl.pallas_call(functools.partial(kernel, n, chips, layers), out_shape=[pl...  156 us
    pallas_call x1, Pallas kernels, step(): pl.pallas_call(functools.partial(write, n), out_shape=[jax.ShapeDtypeStru...  6.69 us

profile of v12, /device:TPU:21, one launch (start us, length us, event | category | flops | bytes accessed | tf_op | source)
XLA Modules:
  0.0 163.0 jit_solution(6108332507442340971)
XLA Ops:
  0.6 155.7 %step.1 = (bf16[2,8,2,5,8,2048]{5,4,3,2,1,0:T(8,128)(2,1)S(1)}, bf16[2,8,2,5,8,2048]{5,4,3,2,1,0:T(8,128)(2,1)S(1)}, bf16[2,8,2,16,8,640]{5,4,3,2,1,0:T(8,128)(2...) custom-call(bf16[2,8,2,5,8,2048]{5,4,3,2,1,0:T(8,128)(2,1)} %bitcast, ...), custom_call_target="tpu_custom_call" | custom-call | tf_op jit(solution)/shard_map/step/pallas_call | solution.py:426
  156.4 6.7 %write.1 = (bf16[2,8,2,5,8,2048]{5,4,3,2,1,0:T(8,128)(2,1)}, bf16[2,8,2,5,8,2048]{5,4,3,2,1,0:T(8,128)(2,1)}, bf16[2,8,2,16,8,640]{5,4,3,2,1,0:T(8,128)(2,1)}, f...) custom-call(bf16[2,8,2,5,8,2048]{5,4,3,2,1,0:T(8,128)(2,1)S(1)} %get, ...), custom_call_target="tpu_custom_call" | custom-call | tf_op jit(solution)/shard_map/write/pallas_call | solution.py:457

commit v13 on v12

--- a/solution.py
+++ b/solution.py
@@ -11,7 +11,7 @@
 CORES = 2
 SUBLANES = 8
 HEAD = 1
-PARTS = 2
+PARTS = 3
 SEAM = 10
 LIFT = 12
 DETOUR = (12, 4)

time: 163 us -> 163 us (level)
  no operation moved by 1% of the time
where the time goes in v13:
time: 163 us
  Pallas kernels  162 us (99%)
    pallas_call x1, Pallas kernels, step(): pl.pallas_call(functools.partial(kernel, n, chips, layers), out_shape=[pl...  156 us
    pallas_call x1, Pallas kernels, step(): pl.pallas_call(functools.partial(write, n), out_shape=[jax.ShapeDtypeStru...  6.69 us

profile of v13, /device:TPU:21, one launch (start us, length us, event | category | flops | bytes accessed | tf_op | source)
XLA Modules:
  0.0 163.1 jit_solution(8231554241926841348)
XLA Ops:
  0.6 155.7 %step.1 = (bf16[2,8,2,5,8,2048]{5,4,3,2,1,0:T(8,128)(2,1)S(1)}, bf16[2,8,2,5,8,2048]{5,4,3,2,1,0:T(8,128)(2,1)S(1)}, bf16[2,8,2,16,8,640]{5,4,3,2,1,0:T(8,128)(2...) custom-call(bf16[2,8,2,5,8,2048]{5,4,3,2,1,0:T(8,128)(2,1)} %bitcast, ...), custom_call_target="tpu_custom_call" | custom-call | tf_op jit(solution)/shard_map/step/pallas_call | solution.py:426
  156.4 6.7 %write.1 = (bf16[2,8,2,5,8,2048]{5,4,3,2,1,0:T(8,128)(2,1)}, bf16[2,8,2,5,8,2048]{5,4,3,2,1,0:T(8,128)(2,1)}, bf16[2,8,2,16,8,640]{5,4,3,2,1,0:T(8,128)(2,1)}, f...) custom-call(bf16[2,8,2,5,8,2048]{5,4,3,2,1,0:T(8,128)(2,1)S(1)} %get, ...), custom_call_target="tpu_custom_call" | custom-call | tf_op jit(solution)/shard_map/write/pallas_call | solution.py:457
